TPU v7x, 32 devices: a whole 2x2x4 slice. The times are simulated.
32 devices in a mesh: bond: 8 (over z, x), row: 4 (over y, core).
Axes of the slice: x: 2, y: 2, z: 4, core: 2. Of those that a mesh axis runs over, the one named last changes fastest.
Arguments:
- left_site: bfloat16 [16384, 1024], P(('bond', 'row')), may hold values from -6 to 6
- right_site: bfloat16 [8192, 2048], P(('bond', 'row')), may hold values from -0.1875 to 0.1875
- gate: float32 [4, 4], replicated, may hold values from -3 to 3
- omega: bfloat16 [2048, 1024], P(('bond', 'row')), may hold values from -0.125 to 0.125
Outputs:
- left_new: bfloat16 [16384, 1024], P(('bond', 'row'))
- right_new: bfloat16 [8192, 2048], P(('bond', 'row'))
- odd_pair: bfloat16 [16384, 2048], P(('bond', 'row'))
All inputs are finite; a program needn't handle non-finite values.
Results may differ from a plain program's by a relative error of at most 0.03.
Values may be sent and summed in bfloat16 or wider, within the bound.
A program may use at most 128 MiB of HBM per device.

v0:
```python
import functools
import math

import jax
import jax.numpy as jnp
from jax import lax
from jax.experimental import pallas as pl
from jax.experimental.pallas import tpu as pltpu
from jax.sharding import PartitionSpec as P

LANES = 128
SUB = 8


MESH = pl.DeviceIdType.MESH
CHUNKS = 8


def partner(me, distance):
    span = 2 * distance
    return lax.div(me, span) * span + lax.rem(lax.rem(me, span) + distance, span)


def distances(n):
    found = []
    while n > 1:
        n //= 2
        found.append(n)
    return found


def gather_kernel(axis, n, last, block_ref, out_ref, send_sem, recv_sem):
    shifted = last is not None
    me = lax.axis_index(axis)
    rows = block_ref.shape[0]
    piece = rows // CHUNKS
    steps = distances(n)

    barrier = pltpu.get_barrier_semaphore()
    for s in steps:
        pl.semaphore_signal(barrier, inc=1, device_id={axis: partner(me, s)}, device_id_type=MESH)
    if shifted:
        bond = lax.axis_index("bond")
        for way in (1, last):
            to = lax.rem(bond + way, last + 1)
            pl.semaphore_signal(barrier, inc=1, device_id={"bond": to}, device_id_type=MESH)
    pl.semaphore_wait(barrier, len(steps) + (2 if shifted else 0))

    def owner(mask):
        at = me
        for s in steps:
            if mask & s:
                at = partner(at, s)
        return at

    def slot(mask, k):
        start = pl.multiple_of(owner(mask) * rows + k * piece, piece)
        return out_ref.at[pl.ds(start, piece), :]

    def own(k):
        return block_ref.at[k * piece:(k + 1) * piece, :]

    def copy(mask, s, k):
        source = slot(mask, k) if mask or shifted else own(k)
        return pltpu.make_async_remote_copy(
            src_ref=source,
            dst_ref=slot(mask, k),
            send_sem=send_sem.at[mask + s, k],
            recv_sem=recv_sem.at[mask + s, k],
            device_id={axis: partner(me, s)},
            device_id_type=MESH,
        )

    def behind(k):
        return pltpu.make_async_remote_copy(
            src_ref=own(k),
            dst_ref=slot(0, k),
            send_sem=send_sem.at[0, k],
            recv_sem=recv_sem.at[0, k],
            device_id={"bond": bond - 1},
            device_id_type=MESH,
        )

    def lower_steps(mask):
        return [s for s in steps if mask == 0 or s < (mask & -mask)]

    order = [m for s in steps for m in range(s, n, 2 * s)]

    def spread():
        for s in steps:
            for k in range(CHUNKS):
                if shifted and s == steps[0]:
                    behind(k).wait_recv()
                copy(0, s, k).start()
        for mask in order:
            for k in range(CHUNKS):
                copy(mask - (mask & -mask), mask & -mask, k).wait_recv()
                for s in lower_steps(mask):
                    copy(mask, s, k).start()
        for mask in [0] + order:
            for s in lower_steps(mask):
                for k in range(CHUNKS):
                    copy(mask, s, k).wait_send()

    if not shifted:
        start = pl.multiple_of(me * rows, rows)
        spread()
        out_ref[pl.ds(start, rows), :] = block_ref[...]
        return

    @pl.when(bond > 0)
    def _():
        for k in range(CHUNKS):
            behind(k).start()

    @pl.when(bond < last)
    def _():
        spread()

    @pl.when(bond == last)
    def _():
        out_ref[...] = jnp.zeros_like(out_ref)

    @pl.when(bond > 0)
    def _():
        for k in range(CHUNKS):
            behind(k).wait_send()


def gather(block, axis, n, last, number):
    rows, columns = block.shape
    return pl.pallas_call(
        functools.partial(gather_kernel, axis, n, last),
        out_shape=jax.ShapeDtypeStruct((n * rows, columns), block.dtype),
        in_specs=[pl.BlockSpec(memory_space=pltpu.VMEM)],
        out_specs=pl.BlockSpec(memory_space=pltpu.VMEM),
        scratch_shapes=[pltpu.SemaphoreType.DMA((n, CHUNKS)), pltpu.SemaphoreType.DMA((n, CHUNKS))],
        compiler_params=pltpu.CompilerParams(
            collective_id=number, has_side_effects=True, vmem_limit_bytes=16 * 1024 * 1024
        ),
        cost_estimate=pl.CostEstimate(flops=0, bytes_accessed=100 * 1024 * 1024, transcendentals=0),
        name="gather",
    )(block)


def split(x):
    high = x.astype(jnp.bfloat16)
    return high, (x - high.astype(jnp.float32)).astype(jnp.bfloat16)


def inverse_factor(block):
    groups = LANES // SUB
    lane = lax.broadcasted_iota(jnp.int32, (SUB, LANES), 1)
    sub = lax.broadcasted_iota(jnp.int32, (SUB, LANES), 0)
    left = [block[g * SUB:(g + 1) * SUB, :] for g in range(groups)]
    right = [jnp.where(lane == sub + g * SUB, 1.0, 0.0) for g in range(groups)]
    rows = []

    def over_lanes(x, column):
        return jnp.broadcast_to(x[:, column:column + 1], (SUB, LANES))

    def over_rows(x, row):
        return jnp.broadcast_to(x[row:row + 1, :], (SUB, LANES))

    for g in range(groups):
        a, e = left[g], right[g]
        cols = [over_lanes(a, g * SUB + c) for c in range(SUB)]
        finished = jnp.zeros_like(e)
        for k in range(SUB):
            here = sub == k
            pivot = over_rows(cols[k], k)
            inverse = 1.0 / pivot
            factor = cols[k] * inverse
            row_a, row_e = over_rows(a, k), over_rows(e, k)
            finished = jnp.where(here, row_e * lax.rsqrt(pivot), finished)
            a = jnp.where(here, row_a * inverse, a - factor * row_a)
            e = jnp.where(here, row_e * inverse, e - factor * row_e)
            for c in range(k + 1, SUB):
                row_c = over_rows(cols[c], k)
                cols[c] = jnp.where(here, row_c * inverse, cols[c] - factor * row_c)
        rows.append(finished)
        if g + 1 == groups:
            break
        wide_a = [over_rows(a, k) for k in range(SUB)]
        wide_e = [over_rows(e, k) for k in range(SUB)]
        for i in range(g + 1, groups):
            coeff = [over_lanes(left[i], g * SUB + c) for c in range(SUB)]
            for c in range(SUB):
                left[i] = left[i] - coeff[c] * wide_a[c]
                right[i] = right[i] - coeff[c] * wide_e[c]
    return jnp.concatenate(rows, axis=0)


def add_up(n, gram_ref, work, near, far, sums, others, send_sem, recv_sem):
    size = gram_ref.shape[0]
    blocks, half = size // LANES, LANES // 2
    me = lax.axis_index("row")
    steps = distances(n)[::-1]
    mine = lax.rem(me, 2)

    barrier = pltpu.get_barrier_semaphore()
    for s in steps:
        pl.semaphore_signal(barrier, inc=1, device_id={"row": partner(me, s)}, device_id_type=MESH)
    pl.semaphore_wait(barrier, len(steps))

    def rows(i, side):
        return pl.ds(pl.multiple_of(i * LANES + side * half, half), half)

    def copy(source, target, stage, s, i):
        return pltpu.make_async_remote_copy(
            src_ref=source,
            dst_ref=target,
            send_sem=send_sem.at[stage, i],
            recv_sem=recv_sem.at[stage, i],
            device_id={"row": partner(me, s)},
            device_id_type=MESH,
        )

    def packed(ref, i):
        return ref.at[i * half:(i + 1) * half, i * LANES:]

    def first(i):
        return copy(gram_ref.at[rows(i, 1 - mine), i * LANES:], packed(near, i), 0, 1, i)

    def across(j, i):
        return copy(packed(sums, i), packed(far.at[j], i), j + 1, steps[j + 1], i)

    def back(i):
        return copy(packed(sums, i), packed(others, i), len(steps), 1, i)

    for i in range(blocks):
        first(i).start()
    for i in range(blocks):
        first(i).wait()
        packed(sums, i)[...] = gram_ref[rows(i, mine), i * LANES:] + packed(near, i)[...]
        if len(steps) > 1:
            across(0, i).start()
        else:
            back(i).start()
    for j in range(len(steps) - 1):
        for i in range(blocks):
            across(j, i).wait()
            packed(sums, i)[...] = packed(sums, i)[...] + packed(far.at[j], i)[...]
            if j + 2 < len(steps):
                across(j + 1, i).start()
            else:
                back(i).start()
    for i in range(blocks):
        back(i).wait()
        work[rows(i, mine), i * LANES:size] = packed(sums, i)[...]
        work[rows(i, 1 - mine), i * LANES:size] = packed(others, i)[...]


def solve_kernel(scale, n, gram_ref, sketch_ref, flat_ref, tall_ref, work, wide, *exchange):
    size = gram_ref.shape[0]
    blocks = size // LANES
    width = size + sketch_ref.shape[1]
    eye = (
        lax.broadcasted_iota(jnp.int32, (LANES, LANES), 0)
        == lax.broadcasted_iota(jnp.int32, (LANES, LANES), 1)
    )

    for d in range(1, blocks):
        work[d * LANES:(d + 1) * LANES, :d * LANES] = jnp.zeros((LANES, d * LANES), jnp.float32)
    work[:, size:] = sketch_ref[...]
    add_up(n, gram_ref, work, *exchange)
    total = jnp.zeros((LANES, LANES), jnp.float32)
    for d in range(blocks):
        at = slice(d * LANES, (d + 1) * LANES)
        total = total + jnp.where(eye, work[at, at], 0.0)
    ridge = jnp.sum(total, keepdims=True) * (scale * 0.01 / size)
    for d in range(blocks):
        at = slice(d * LANES, (d + 1) * LANES)
        work[at, d * LANES:size] = work[at, d * LANES:size] * scale
        work[at, at] = work[at, at] + jnp.where(eye, ridge, 0.0)

    def eliminate(d, carry):
        start = pl.multiple_of(d * LANES, LANES)
        here = pl.ds(start, LANES)
        inverse = inverse_factor(work[here, here])
        high, low = split(inverse)
        factor = jnp.concatenate([high, high, low], axis=1)
        high, low = split(work[here, :])
        solved = jnp.dot(
            factor,
            jnp.concatenate([high, low, high], axis=0),
            preferred_element_type=jnp.float32,
        )
        work[here, :] = solved
        high, low = split(solved)
        wide[0:LANES, :] = high
        wide[LANES:2 * LANES, :] = low
        wide[2 * LANES:, :] = high
        basis = solved[:, size:]
        flat_ref[here, :] = basis.astype(jnp.bfloat16)
        tall_ref[:, here] = basis.T.astype(jnp.bfloat16)

        def update(i, carry):
            there = pl.ds(pl.multiple_of(i * LANES, LANES), LANES)
            high, low = split(work[here, there].T)
            lower = jnp.concatenate([high, high, low], axis=1)
            work[there, :] = work[there, :] - jnp.dot(
                lower, wide[...], preferred_element_type=jnp.float32
            )
            return carry

        return lax.fori_loop(d + 1, blocks, update, carry)

    lax.fori_loop(0, blocks, eliminate, 0)


def solve(gram, sketch_t, scale, n, number):
    size, rows = sketch_t.shape
    stages = len(distances(n)) + 1
    packed = (size // 2, size)
    return pl.pallas_call(
        functools.partial(solve_kernel, scale, n),
        out_shape=(
            jax.ShapeDtypeStruct((size, rows), jnp.bfloat16),
            jax.ShapeDtypeStruct((rows, size), jnp.bfloat16),
        ),
        in_specs=[pl.BlockSpec(memory_space=pltpu.VMEM)] * 2,
        out_specs=(pl.BlockSpec(memory_space=pltpu.VMEM),) * 2,
        scratch_shapes=[
            pltpu.VMEM((size, size + rows), jnp.float32),
            pltpu.VMEM((3 * LANES, size + rows), jnp.bfloat16),
            pltpu.VMEM(packed, jnp.float32),
            pltpu.VMEM((max(stages - 2, 1),) + packed, jnp.float32),
            pltpu.VMEM(packed, jnp.float32),
            pltpu.VMEM(packed, jnp.float32),
            pltpu.SemaphoreType.DMA((stages, size // LANES)),
            pltpu.SemaphoreType.DMA((stages, size // LANES)),
        ],
        compiler_params=pltpu.CompilerParams(
            collective_id=number, has_side_effects=True, vmem_limit_bytes=48 * 1024 * 1024
        ),
        cost_estimate=pl.CostEstimate(
            flops=4 * size * size * (size + rows), bytes_accessed=4 * size * (size + 2 * rows), transcendentals=size
        ),
        name="solve",
    )(gram, sketch_t)


def shards(left_site, right_site, gate, omega):
    row_count = left_site.shape[0]
    bond_width = left_site.shape[1]
    kept_rank = omega.shape[1]
    group = lax.axis_size("row")
    product = jnp.dot(
        left_site,
        gather(right_site, "row", group, None, 0),
        preferred_element_type=jnp.float32,
    )
    mixed = jnp.einsum(
        "stuv,auvc->astc",
        gate.reshape(2, 2, 2, 2),
        product.reshape(row_count // 2, 2, 2, bond_width),
    )
    theta = mixed.reshape(row_count, 2 * bond_width).astype(jnp.bfloat16)
    sketch_t = lax.dot_general(
        lax.all_gather(omega, ("bond", "row"), axis=0, tiled=True),
        theta,
        (((0,), (1,)), ((), ())),
        preferred_element_type=jnp.float32,
    )
    high, low = split(sketch_t)
    over = (((1,), (1,)), ((), ()))
    local_gram = lax.dot_general(
        jnp.concatenate([high, high, low], axis=1),
        jnp.concatenate([high, low, high], axis=1),
        over,
        preferred_element_type=jnp.float32,
    )
    left_t, left_new = solve(local_gram, sketch_t, 1.0 / (2.0 * bond_width), group, 1)
    right_scale = 1.0 / math.sqrt(2.0 * bond_width)
    own_rows = kept_rank // group
    partial = (jnp.dot(left_t, theta, preferred_element_type=jnp.float32) * right_scale).astype(jnp.bfloat16)
    partial, ahead = lax.optimization_barrier((partial, left_new))
    right_new = lax.psum_scatter(partial, "row", scatter_dimension=0, tiled=True)
    following = gather(
        ahead.reshape(row_count // 2, 2 * kept_rank), "row", group, lax.axis_size("bond") - 1, 2
    )
    right_view = right_new.reshape(2 * own_rows, bond_width)
    pair_sum = jnp.dot(
        right_view,
        following,
        preferred_element_type=jnp.float32,
    )
    odd_pair = (pair_sum * (1.0 / math.sqrt(1.0 * bond_width))).astype(jnp.bfloat16)
    return (left_new, right_new, odd_pair)


def solution(mesh):
    placed = (P(("bond", "row"), None), P(("bond", "row"), None), P(), P(("bond", "row"), None))
    return jax.shard_map(
        shards,
        mesh=mesh,
        in_specs=placed,
        out_specs=(P(("bond", "row"), None), P(("bond", "row"), None), P(("bond", "row"), None)),
        check_vma=False,
    )
```

profile of v0, /device:TPU:1, one launch (start us, length us, event | category | flops | bytes accessed | tf_op | source)
XLA Modules:
  0.0 246.8 jit_solution(3737240624305382497)
XLA Ops:
  7.2 0.0 copy-start
  7.2 0.0 all-gather.2.cloned.1.call-start
  7.2 0.7 all-gather.2.cloned.1.call-update
  7.9 0.0 reduce-scatter.2.cloned.1.call-start
  8.0 0.0 copy-start.2
  8.0 1.2 copy-done.2
  9.2 29.3 %gather.2 = bf16[1024,2048]{1,0:T(8,128)(2,1)S(1)} custom-call(bf16[256,2048]{1,0:T(8,128)(2,1)S(1)} %copy-done.2), custom_call_target="tpu_custom_call" | custom-call | bytes 104857600 | tf_op jit(solution)/shard_map/gather/pallas_call | solution.py:132
  38.5 0.0 copy-done
  38.5 3.7 %fusion.16 = bf16[512,2048]{1,0:T(8,128)(2,1)} fusion(bf16[512,1024]{1,0:T(8,128)(2,1)S(1)} %copy-done, bf16[1024,2048]{1,0:T(8,128)(2,1)S(1)} %gather.2), kind=kOutput, calls=%fused_computation.19 | convolution fusion | flops 2147483648 | bytes 7340032 | tf_op jit(solution)/shard_map/dot_general | solution.py:349
  42.2 0.0 copy-start.5
  42.2 3.3 %reshape.24 = bf16[256,2,2,1024,1]{3,2,1,0,4:T(2,128)(2,1)S(1)} reshape(bf16[512,2048]{1,0:T(8,128)(2,1)} %fusion.16) | data formatting | bytes 4194304 | tf_op jit(solution)/shard_map/reshape | solution.py:357
  45.5 0.0 copy-done.5
  45.5 0.1 reshape.21
  45.6 3.6 %bitcast_convert_fusion = bf16[256,1024,2,2]{1,3,2,0:T(2,128)(2,1)S(1)} fusion(bf16[256,2,2,1024,1]{3,2,1,0,4:T(2,128)(2,1)S(1)} %reshape.24, bf16[2,2,2,2]{3,2,1,0:T(2,128)(2,1)S(1)} %reshape.21), kind=kOutput, calls=%fused_computation.1 | convolution fusion | flops 8388608 | bytes 4194336 | tf_op jit(solution)/shard_map/stuv,auvc->astc/dot_general | solution.py:354
  49.2 0.6 copy.12
  49.8 0.0 copy-start.3
  49.9 25.8 %all-gather.2.cloned.1.call-done = bf16[2048,1024]{1,0:T(8,128)(2,1)} async-done(((bf16[64,1024]{1,0:T(8,128)(2,1)}), bf16[2048,1024]{1,0:T(8,128)(2,1)}) %all-gather.2.cloned.1.call-update) | async-done | bytes 4194320 | tf_op jit(solution)/shard_map/all_gather | solution.py:361
  75.6 4.6 %subtract_convert_fusion = (bf16[1024,512]{1,0:T(8,128)(2,1)S(1)}, bf16[1024,512]{1,0:T(8,128)(2,1)S(1)}, f32[1024,512]{1,0:T(8,128)S(1)}) fusion(bf16[512,2048]{1,0:T(8,128)(2,1)S(1)} %bitcast.25, bf16[2048,1024]{1,0:T(8,128)(2,1)} %all-gather.2.cloned.1.call-done), kind=kOutput, calls=%fused_computation.14 | convolution fusion | flops 2149580800 | bytes 10485760 | tf_op jit(solution)/shard_map/dot_general | solution.py:360
  80.2 0.0 copy-done.3
  80.2 5.4 %fusion.5.gram_ref = f32[1024,1024]{1,0:T(8,128)} fusion(bf16[1024,512]{1,0:T(8,128)(2,1)S(1)} %get-tuple-element.12, bf16[1024,512]{1,0:T(8,128)(2,1)S(1)} %get-tuple-element.11), kind=kOutput, calls=%fused_computation.8 | convolution fusion | flops 3240099840 | bytes 6291456 | tf_op jit(solution)/shard_map/dot_general | solution.py:368
  85.6 0.0 copy-start.4
  85.6 86.4 %solve.1 = (bf16[1024,512]{1,0:T(8,128)(2,1)S(1)}, bf16[512,1024]{1,0:T(8,128)(2,1)S(1)}) custom-call(f32[1024,1024]{1,0:T(8,128)} %fusion.5.gram_ref, f32[1024,512]{1,0:T(8,128)S(1)} %get-tuple-element.13.sketch_ref), custom_call_target="tpu_custom_call" | custom-call | flops 6442450944 | bytes 8388608 | tf_op jit(solution)/shard_map/solve/pallas_call | solution.py:316
  172.0 0.0 copy-done.4
  172.0 4.3 %multiply_convert_fusion = bf16[1024,2048]{1,0:T(8,128)(2,1)} fusion(bf16[1024,512]{1,0:T(8,128)(2,1)S(1)} %get-tuple-element.8, bf16[512,2048]{1,0:T(8,128)(2,1)S(1)} %bitcast.26), kind=kOutput, calls=%fused_computation | convolution fusion | flops 2151677952 | bytes 7340032 | tf_op jit(solution)/shard_map/dot_general | solution.py:377
  176.3 0.0 reduce-scatter.2.cloned.1.call-update
  176.3 0.4 reshape.23.block_ref
  176.7 46.2 %gather.3 = bf16[1024,2048]{1,0:T(8,128)(2,1)S(1)} custom-call(bf16[256,2048]{1,0:T(8,128)(2,1)S(1)} %reshape.23.block_ref), custom_call_target="tpu_custom_call" | custom-call | bytes 104857600 | tf_op jit(solution)/shard_map/gather/pallas_call | solution.py:132
  222.9 0.0 copy-start.1
  222.9 2.0 copy-done.1
  224.9 6.8 %reduce-scatter.2.cloned.1.call-done = bf16[256,2048]{1,0:T(8,128)(2,1)} async-done(((bf16[1024,2048]{1,0:T(8,128)(2,1)}), bf16[256,2048]{1,0:T(8,128)(2,1)}) %reduce-scatter.2.cloned.1.call-update) | async-done | bytes 1048592 | tf_op jit(solution)/shard_map/reduce_scatter | solution.py:379
  231.7 1.4 reshape.22
  233.1 5.8 %multiply_convert_fusion.1 = bf16[512,2048]{1,0:T(8,128)(2,1)} fusion(bf16[512,1024]{1,0:T(8,128)(2,1)S(1)} %reshape.22, bf16[1024,2048]{1,0:T(8,128)(2,1)} %copy-done.1), kind=kOutput, calls=%fused_computation.4 | convolution fusion | flops 2149580800 | bytes 7340032 | tf_op jit(solution)/shard_map/dot_general | solution.py:384
  238.9 1.0 copy.18
Async XLA Ops:
  7.2 31.3 %copy-start = (bf16[512,1024]{1,0:T(8,128)(2,1)S(1)}, bf16[512,1024]{1,0:T(8,128)(2,1)}, u32[]{:S(2)}) copy-start(bf16[512,1024]{1,0:T(8,128)(2,1)} %param.4) | copy-start | bytes 3145732
  7.2 68.5 %all-gather.2.cloned.1.call-start = ((), (), s32[]{:S(2)}) async-start(), calls=%async_computation.1 | async-start | bytes 4325376 | tf_op jit(solution)/shard_map/all_gather | solution.py:361
  7.9 223.8 %reduce-scatter.2.cloned.1.call-start = ((), (), s32[]{:S(2)}) async-start(), calls=%async_computation.2 | async-start | bytes 5242880 | tf_op jit(solution)/shard_map/reduce_scatter | solution.py:379
  8.0 1.2 copy-start.2
  42.2 3.3 %copy-start.5 = (f32[4,4]{1,0:T(4,128)S(1)}, f32[4,4]{1,0:T(4,128)}, u32[]{:S(2)}) copy-start(f32[4,4]{1,0:T(4,128)} %param.6) | copy-start | bytes 196
  49.8 30.4 %copy-start.3 = (bf16[64,8,2,1024]{3,1,2,0:T(8,128)(2,1)}, bf16[64,8,2,1024]{3,1,2,0:T(8,128)(2,1)S(1)}, u32[]{:S(2)}) copy-start(bf16[64,8,2,1024]{3,1,2,0:T(8,128)(2,1)S(1)} %copy.12) | copy-start | bytes 6291460
  85.6 86.4 %copy-start.4 = (bf16[64,8,2,1024]{3,1,2,0:T(8,128)(2,1)S(1)}, bf16[64,8,2,1024]{3,1,2,0:T(8,128)(2,1)}, u32[]{:S(2)}) copy-start(bf16[64,8,2,1024]{3,1,2,0:T(8,128)(2,1)} %copy-done.3) | copy-start | bytes 6291460
  222.9 2.0 copy-start.1
Sparse Core Ops, SparseCore 0:
  10.9 64.7 all-gather.1
  176.5 55.1 reduce-scatter.1
where the time goes:
time: 248 us; the launch traced here: 247 us
  Pallas kernels  162 us (65%)
  waiting for transfers between devices  33.2 us (13%)
  matrix products  27.4 us (11%)
  between operations  14.2 us (6%)
  local copies, waits for them, and re-layouts  9.97 us (4%)
    pallas_call x1, Pallas kernels, solve(): pl.pallas_call(functools.partial(solve_kernel, scale, n), out_shape=(jax....  86.4 us
    pallas_call x2, Pallas kernels, gather(): pl.pallas_call(functools.partial(gather_kernel, axis, n, last), out_shape...  75.5 us
    all_gather x1, waiting for transfers between devices, shards(): lax.all_gather(omega, ('bond', 'row'), axis=0, tiled=True)  25.8 us
    reduce_scatter x1, waiting for transfers between devices, shards(): lax.psum_scatter(partial, 'row', scatter_dimension=0, tiled=True)  6.77 us
    dot_general x1, matrix products, shards(): jnp.dot(right_view, following, preferred_element_type=jnp.float32)  5.85 us
    dot_general x1, matrix products, shards(): lax.dot_general(jnp.concatenate([high, high, low], axis=1), jnp.concatena...  5.41 us
  transfers between devices with their start and end apart: 2, of which 2 were waited for; matrix products, arithmetic and copies ran while one was open for 5% of the time, Pallas kernels for 31%

commit v1 on v0

v1 whole, which is shorter than its diff:
```python
import functools
import math

import jax
import jax.numpy as jnp
from jax import lax
from jax.experimental import pallas as pl
from jax.experimental.pallas import tpu as pltpu
from jax.sharding import PartitionSpec as P

LANES = 128
SUB = 8
TILE = 256
PARTS = 2
CHUNKS = 8
MESH = pl.DeviceIdType.MESH
F32 = jnp.float32
BF16 = jnp.bfloat16


def partner(me, distance):
    span = 2 * distance
    return lax.div(me, span) * span + lax.rem(lax.rem(me, span) + distance, span)


def distances(n):
    found = []
    while n > 1:
        n //= 2
        found.append(n)
    return found


def split(x):
    high = x.astype(BF16)
    return high, (x - high.astype(F32)).astype(BF16)


def dot(a, b):
    return jnp.dot(a, b, preferred_element_type=F32)


def inverse_factor(block):
    groups = LANES // SUB
    lane = lax.broadcasted_iota(jnp.int32, (SUB, LANES), 1)
    sub = lax.broadcasted_iota(jnp.int32, (SUB, LANES), 0)
    left = [block[g * SUB:(g + 1) * SUB, :] for g in range(groups)]
    right = [jnp.where(lane == sub + g * SUB, 1.0, 0.0) for g in range(groups)]
    rows = []

    def over_lanes(x, column):
        return jnp.broadcast_to(x[:, column:column + 1], (SUB, LANES))

    def over_rows(x, row):
        return jnp.broadcast_to(x[row:row + 1, :], (SUB, LANES))

    for g in range(groups):
        a, e = left[g], right[g]
        cols = [over_lanes(a, g * SUB + c) for c in range(SUB)]
        finished = jnp.zeros_like(e)
        for k in range(SUB):
            here = sub == k
            root = lax.rsqrt(over_rows(cols[k], k))
            inverse = root * root
            factor = cols[k] * inverse
            row_a, row_e = over_rows(a, k), over_rows(e, k)
            finished = jnp.where(here, row_e * root, finished)
            a = jnp.where(here, row_a * inverse, a - factor * row_a)
            e = jnp.where(here, row_e * inverse, e - factor * row_e)
            for c in range(k + 1, SUB):
                row_c = over_rows(cols[c], k)
                cols[c] = jnp.where(here, row_c * inverse, cols[c] - factor * row_c)
        rows.append(finished)
        if g + 1 == groups:
            break
        wide_a = [over_rows(a, k) for k in range(SUB)]
        wide_e = [over_rows(e, k) for k in range(SUB)]
        for i in range(g + 1, groups):
            coeff = [over_lanes(left[i], g * SUB + c) for c in range(SUB)]
            for c in range(SUB):
                left[i] = left[i] - coeff[c] * wide_a[c]
                right[i] = right[i] - coeff[c] * wide_e[c]
    return jnp.concatenate(rows, axis=0)


def layer_kernel(
    n, bonds, gate_ref, a_ref, b_ref, omega_ref, left_ref, right_ref, odd_ref,
    a_all, b_all, omega_all, theta, w_row, w_tall, work, gram_own, gram_in, panel, wide,
    flat, ahead, right_out, right_in, right_own, right_view, trace_own, trace_in,
    omega_send, omega_recv, b_send, b_recv, a_send, a_recv, gram_send, gram_recv, trace_send, trace_recv,
    shift_send, shift_recv, far_send, far_recv, near_send, near_recv, right_send, right_recv,
):
    bond, me = lax.axis_index("bond"), lax.axis_index("row")
    last = bonds - 1
    slots = n // 2
    slot, parity = lax.div(me, 2), lax.rem(me, 2)
    near = partner(me, 1)
    bond_dim = a_ref.shape[2]
    rank = omega_ref.shape[1]
    part_rows = a_ref.shape[1]
    block_rows = PARTS * part_rows
    half = block_rows // 2
    own_rank = rank // n
    blocks = rank // LANES
    depth = b_ref.shape[0]
    piece = depth // CHUNKS
    drawn = omega_ref.shape[0]

    def peer(j):
        return 2 * lax.rem(slot + j, slots) + parity

    def source(j, side):
        return 2 * lax.rem(slot + slots - j, slots) + side

    row_steps, bond_steps = distances(n), distances(bonds)

    barrier = pltpu.get_barrier_semaphore()
    greeted = 0
    for j in range(1, n):
        to = lax.rem(me + j, n)
        pl.semaphore_signal(barrier, inc=1, device_id={"row": to}, device_id_type=MESH)
        greeted += 1
    for s in bond_steps:
        pl.semaphore_signal(barrier, inc=1, device_id={"bond": partner(bond, s)}, device_id_type=MESH)
        greeted += 1
    for way in (1, last):
        to = lax.rem(bond + way, bonds)
        pl.semaphore_signal(barrier, inc=1, device_id={"bond": to}, device_id_type=MESH)
        greeted += 1
    pl.semaphore_wait(barrier, greeted)

    hops = [("row", s) for s in row_steps[:-1]] + [("bond", s) for s in bond_steps] + [("row", 1)]
    bits = [1 << (len(hops) - 1 - i) for i in range(len(hops))]
    hop_of = dict(zip(bits, hops))

    def whose(mask):
        at = {"row": me, "bond": bond}
        for bit in bits:
            if mask & bit:
                axis, s = hop_of[bit]
                at[axis] = partner(at[axis], s)
        return at["bond"] * n + at["row"]

    def omega_slot(mask):
        return omega_all.at[pl.ds(pl.multiple_of(whose(mask) * drawn, drawn), drawn), :]

    def omega_copy(mask, bit):
        axis, s = hop_of[bit]
        to = partner(me if axis == "row" else bond, s)
        return pltpu.make_async_remote_copy(
            src_ref=omega_slot(mask) if mask else omega_ref,
            dst_ref=omega_slot(mask),
            send_sem=omega_send.at[mask + bit],
            recv_sem=omega_recv.at[mask + bit],
            device_id={axis: to},
            device_id_type=MESH,
        )

    def lower_bits(mask):
        return [bit for bit in bits if mask == 0 or bit < (mask & -mask)]

    omega_order = [m for bit in bits for m in range(bit, 2 * bits[0], 2 * bit)]

    def b_copy(mask, s, k):
        at = me
        for step in row_steps:
            if mask & step:
                at = partner(at, step)
        start = pl.multiple_of(at * depth + k * piece, piece)
        target = b_all.at[pl.ds(start, piece), :]
        return pltpu.make_async_remote_copy(
            src_ref=target if mask else b_ref.at[k * piece:(k + 1) * piece, :],
            dst_ref=target,
            send_sem=b_send.at[mask + s, k],
            recv_sem=b_recv.at[mask + s, k],
            device_id={"row": partner(me, s)},
            device_id_type=MESH,
        )

    def b_lower(mask):
        return [s for s in row_steps if mask == 0 or s < (mask & -mask)]

    b_order = [m for s in row_steps for m in range(s, n, 2 * s)]

    def a_copy(j, q):
        return pltpu.make_async_remote_copy(
            src_ref=a_ref.at[q],
            dst_ref=a_all.at[slot, q],
            send_sem=a_send.at[j, q],
            recv_sem=a_recv.at[j, q],
            device_id={"row": peer(j)},
            device_id_type=MESH,
        )

    def a_arrival(j, q):
        return pltpu.make_async_remote_copy(
            src_ref=a_ref.at[q],
            dst_ref=a_all.at[lax.rem(slot + slots - j, slots), q],
            send_sem=a_send.at[j, q],
            recv_sem=a_recv.at[j, q],
            device_id={"row": peer(j)},
            device_id_type=MESH,
        )

    for bit in bits:
        omega_copy(0, bit).start()
    for s in row_steps:
        for k in range(CHUNKS):
            b_copy(0, s, k).start()
    for j in range(1, slots):
        for q in range(PARTS):
            a_copy(j, q).start()

    a_all[slot] = a_ref[...]
    b_all[pl.ds(pl.multiple_of(me * depth, depth), depth), :] = b_ref[...]
    omega_all[pl.ds(pl.multiple_of((bond * n + me) * drawn, drawn), drawn), :] = omega_ref[...]

    def clear(i, carry):
        at = pl.ds(pl.multiple_of(i * LANES, LANES), LANES)
        work[at, :] = jnp.zeros((LANES, rank), F32)
        gram_own[at, :] = jnp.zeros((LANES, rank), F32)
        return carry

    lax.fori_loop(0, blocks, clear, 0)

    todo = [(m, k) for m in b_order for k in range(CHUNKS)]
    every = -(-len(omega_order) // len(todo))
    steps = []
    for i, (m, k) in enumerate(todo):
        steps += [("o", o) for o in omega_order[i * every:(i + 1) * every]]
        steps.append(("b", (m, k)))
    for kind, what in steps:
        if kind == "o":
            low = what & -what
            omega_copy(what - low, low).wait_recv()
            for bit in lower_bits(what):
                omega_copy(what, bit).start()
        else:
            m, k = what
            b_copy(m - (m & -m), m & -m, k).wait_recv()
            for s in b_lower(m):
                b_copy(m, s, k).start()

    def mix(index, carry):
        j, q = lax.div(index, PARTS), lax.rem(index, PARTS)
        at = lax.rem(slot + slots - j, slots)

        @pl.when(j > 0)
        def _():
            a_arrival(j, q).wait_recv()

        base = pl.multiple_of((at * PARTS + q) * part_rows, part_rows)
        rows = pl.ds(base, part_rows)
        side = part_rows // 2

        def columns(cb, carry):
            c0 = pl.multiple_of(cb * TILE, TILE)
            c1 = pl.multiple_of(bond_dim + cb * TILE, TILE)
            block = a_all[at, q]
            product = [dot(block, b_all[:, pl.ds(c, TILE)]) for c in (c0, c1)]
            for s in range(2):
                for t in range(2):
                    total = None
                    for u in range(2):
                        for v in range(2):
                            term = gate_ref[2 * s + t, 2 * u + v] * product[v][u * side:(u + 1) * side, :]
                            total = term if total is None else total + term
                    theta[pl.ds(pl.multiple_of(base + s * side, side), side), pl.ds((c0, c1)[t], TILE)] = total.astype(BF16)
            return carry

        lax.fori_loop(0, bond_dim // TILE, columns, 0)

        def sketch(rb, carry):
            at_rank = pl.ds(pl.multiple_of(rb * TILE, TILE), TILE)
            value = dot(theta[rows, :], omega_all[:, at_rank].astype(BF16))
            w_row[rows, at_rank] = value.astype(BF16)
            w_tall[at_rank, rows] = value.T.astype(BF16)
            return carry

        lax.fori_loop(0, rank // TILE, sketch, 0)
        for i in range(rank // TILE):
            mine = slice(i * TILE, (i + 1) * TILE)
            gram_own[mine, i * TILE:] += dot(w_tall[mine, rows], w_row[rows, i * TILE:])
        return carry

    lax.fori_loop(0, slots * PARTS, mix, 0)

    def gram_copy(i):
        at = pl.ds(pl.multiple_of(i * LANES, LANES), LANES)
        return pltpu.make_async_remote_copy(
            src_ref=gram_own.at[at, :],
            dst_ref=gram_in.at[at, :],
            send_sem=gram_send.at[i],
            recv_sem=gram_recv.at[i],
            device_id={"row": near},
            device_id_type=MESH,
        )

    trace_copy = pltpu.make_async_remote_copy(
        src_ref=trace_own,
        dst_ref=trace_in,
        send_sem=trace_send,
        recv_sem=trace_recv,
        device_id={"row": near},
        device_id_type=MESH,
    )
    for i in range(blocks):
        gram_copy(i).start()
    eye = (
        lax.broadcasted_iota(jnp.int32, (LANES, LANES), 0)
        == lax.broadcasted_iota(jnp.int32, (LANES, LANES), 1)
    )
    column = lax.broadcasted_iota(jnp.int32, (LANES, rank), 1)
    total = jnp.zeros((LANES, LANES), F32)
    for d in range(blocks):
        at = slice(d * LANES, (d + 1) * LANES)
        total = total + jnp.where(eye, gram_own[at, at], 0.0)
    trace_own[...] = jnp.broadcast_to(jnp.sum(total, keepdims=True), (SUB, LANES))
    trace_copy.start()
    scale = 1.0 / (2.0 * bond_dim)
    trace_copy.wait()
    ridge = (trace_own[0:1, 0:1] + trace_in[0:1, 0:1]) * (scale * 0.01 / rank)

    def ahead_at(d, who):
        return ahead.at[d, :, pl.ds(pl.multiple_of(who * half, half), half), :]

    def shift_copy(d):
        return pltpu.make_async_remote_copy(
            src_ref=left_ref.at[d],
            dst_ref=ahead_at(d, me),
            send_sem=shift_send.at[d],
            recv_sem=shift_recv.at[d],
            device_id={"bond": lax.max(bond - 1, 0)},
            device_id_type=MESH,
        )

    def far_copy(j, d):
        return pltpu.make_async_remote_copy(
            src_ref=ahead_at(d, me),
            dst_ref=ahead_at(d, me),
            send_sem=far_send.at[j, d],
            recv_sem=far_recv.at[j, d],
            device_id={"row": peer(j)},
            device_id_type=MESH,
        )

    def far_arrival(j, d):
        return pltpu.make_async_remote_copy(
            src_ref=ahead_at(d, me),
            dst_ref=ahead_at(d, source(j, parity)),
            send_sem=far_send.at[j, d],
            recv_sem=far_recv.at[j, d],
            device_id={"row": peer(j)},
            device_id_type=MESH,
        )

    def near_copy(j, d, side):
        return pltpu.make_async_remote_copy(
            src_ref=ahead_at(d, source(j, side)),
            dst_ref=ahead_at(d, source(j, side)),
            send_sem=near_send.at[j, d],
            recv_sem=near_recv.at[j, d],
            device_id={"row": near},
            device_id_type=MESH,
        )

    def pass_on(d):
        shift_copy(d).wait_recv()
        for j in range(1, slots):
            far_copy(j, d).start()
        near_copy(0, d, parity).start()

    def pass_near(d):
        for j in range(1, slots):
            far_arrival(j, d).wait_recv()
            near_copy(j, d, parity).start()

    def eliminate(d, carry):
        start = pl.multiple_of(d * LANES, LANES)
        here = pl.ds(start, LANES)
        gram_copy(d).wait()
        panel[...] = work[here, :] + jnp.where(
            column >= start, (gram_own[here, :] + gram_in[here, :]) * scale, 0.0
        )
        inverse = inverse_factor(panel[:, here] + jnp.where(eye, ridge, 0.0))
        high, low = split(inverse)
        factor = jnp.concatenate([high, high, low], axis=1)
        high, low = split(panel[...])
        panel[...] = dot(factor, jnp.concatenate([high, low, high], axis=0))
        panel[:, here] = inverse
        high, low = split(panel[...])
        wide[0:LANES, :] = high
        wide[LANES:2 * LANES, :] = low
        wide[2 * LANES:, :] = high

        def update(i, carry):
            at = pl.multiple_of(i * LANES, LANES)
            there = pl.ds(at, LANES)
            high, low = split(panel[:, there].T)
            lower = jnp.concatenate([high, high, low], axis=1)
            kept = jnp.where((column >= start) & (column < start + LANES), 0.0, work[there, :])
            work[there, :] = kept - dot(lower, wide[...])
            return carry

        lax.fori_loop(d + 1, blocks, update, 0)

        known = column < start + LANES
        zero = jnp.zeros((LANES, rank), BF16)
        stacked = jnp.concatenate(
            [jnp.where(known, wide[0:LANES, :], zero), jnp.where(known, wide[LANES:2 * LANES, :], zero)], axis=0
        )
        both = dot(stacked, w_tall[...])
        basis = both[:LANES, :] + both[LANES:, :]
        flat[here, :] = basis.astype(BF16)
        side = part_rows // 2
        for q in range(PARTS):
            for s in range(2):
                first = pl.multiple_of(slot * block_rows + q * part_rows + s * side, side)
                left_ref[d, s, q * side:(q + 1) * side, :] = flat[here, pl.ds(first, side)].T

        @pl.when(bond > 0)
        def _():
            shift_copy(d).start()

        @pl.when((bond < last) & (d > 0))
        def _():
            pass_on(d - 1)

        @pl.when((bond < last) & (d > 1))
        def _():
            pass_near(d - 2)

        return carry

    lax.fori_loop(0, blocks, eliminate, 0)

    right_copy = pltpu.make_async_remote_copy(
        src_ref=right_out,
        dst_ref=right_in,
        send_sem=right_send,
        recv_sem=right_recv,
        device_id={"row": near},
        device_id_type=MESH,
    )

    def project(who, target):
        ranks = pl.ds(pl.multiple_of(who * own_rank, own_rank), own_rank)

        def columns(cb, carry):
            at = pl.ds(pl.multiple_of(cb * TILE, TILE), TILE)
            target[:, at] = dot(flat[ranks, :], theta[:, at]).astype(target.dtype)
            return carry

        lax.fori_loop(0, 2 * bond_dim // TILE, columns, 0)

    project(near, right_out)
    right_copy.start()
    project(me, right_own)

    @pl.when(bond < last)
    def _():
        if blocks > 1:
            pass_near(blocks - 2)
        pass_on(blocks - 1)

    right_copy.wait()
    right_scale = 1.0 / math.sqrt(2.0 * bond_dim)
    right_ref[...] = ((right_own[...] + right_in[...].astype(F32)) * right_scale).astype(BF16)

    @pl.when(bond < last)
    def _():
        view_rows = 2 * own_rank
        row = lax.broadcasted_iota(jnp.int32, (view_rows, view_rows), 0)
        col = lax.broadcasted_iota(jnp.int32, (view_rows, view_rows), 1)
        order = jnp.where(col == lax.div(row, 2) + lax.rem(row, 2) * own_rank, 1.0, 0.0).astype(BF16)
        stacked = jnp.concatenate([right_ref[:, :bond_dim], right_ref[:, bond_dim:]], axis=0)
        right_view[...] = dot(order, stacked).astype(BF16)
        odd_scale = 1.0 / math.sqrt(1.0 * bond_dim)

        def pair(d):
            for j in range(slots):
                near_copy(j, d, 1 - parity).wait_recv()
            both = jnp.concatenate([ahead[d, 0], ahead[d, 1]], axis=1)
            value = (dot(right_view[...], both) * odd_scale).astype(BF16)
            odd_ref[:, pl.ds(pl.multiple_of(d * LANES, LANES), LANES)] = value[:, :LANES]
            odd_ref[:, pl.ds(pl.multiple_of(rank + d * LANES, LANES), LANES)] = value[:, LANES:]

        def pairs(d, carry):
            pair(d)
            return carry

        lax.fori_loop(0, blocks - 1, pairs, 0)
        pass_near(blocks - 1)
        pair(blocks - 1)

        def sent(d, carry):
            for j in range(1, slots):
                far_copy(j, d).wait_send()
            for j in range(slots):
                near_copy(j, d, parity).wait_send()
            return carry

        lax.fori_loop(0, blocks, sent, 0)

    @pl.when(bond == last)
    def _():
        odd_ref[...] = jnp.zeros_like(odd_ref)

    @pl.when(bond > 0)
    def _():
        def sent(d, carry):
            shift_copy(d).wait_send()
            return carry

        lax.fori_loop(0, blocks, sent, 0)

    for mask in [0] + omega_order:
        for bit in lower_bits(mask):
            omega_copy(mask, bit).wait_send()
    for mask in [0] + b_order:
        for s in b_lower(mask):
            for k in range(CHUNKS):
                b_copy(mask, s, k).wait_send()
    for j in range(1, slots):
        for q in range(PARTS):
            a_copy(j, q).wait_send()


def layer(gate, left_parts, right_site, omega, n, bonds):
    parts, part_rows, bond_dim = left_parts.shape
    depth = right_site.shape[0]
    drawn, rank = omega.shape
    slots = n // 2
    block_rows = parts * part_rows
    rows = slots * block_rows
    half = block_rows // 2
    own_rank = rank // n
    blocks = rank // LANES
    dma = pltpu.SemaphoreType.DMA
    return pl.pallas_call(
        functools.partial(layer_kernel, n, bonds),
        out_shape=(
            jax.ShapeDtypeStruct((blocks, 2, half, LANES), BF16),
            jax.ShapeDtypeStruct((own_rank, 2 * bond_dim), BF16),
            jax.ShapeDtypeStruct((2 * own_rank, 2 * rank), BF16),
        ),
        in_specs=[pl.BlockSpec(memory_space=pltpu.SMEM)] + [pl.BlockSpec(memory_space=pltpu.VMEM)] * 3,
        out_specs=(pl.BlockSpec(memory_space=pltpu.VMEM),) * 3,
        scratch_shapes=[
            pltpu.VMEM((slots, parts, part_rows, bond_dim), BF16),
            pltpu.VMEM((n * depth, 2 * bond_dim), BF16),
            pltpu.VMEM((bonds * n * drawn, rank), omega.dtype),
            pltpu.VMEM((rows, 2 * bond_dim), BF16),
            pltpu.VMEM((rows, rank), BF16),
            pltpu.VMEM((rank, rows), BF16),
            pltpu.VMEM((rank, rank), F32),
            pltpu.VMEM((rank, rank), F32),
            pltpu.VMEM((rank, rank), F32),
            pltpu.VMEM((LANES, rank), F32),
            pltpu.VMEM((3 * LANES, rank), BF16),
            pltpu.VMEM((rank, rows), BF16),
            pltpu.VMEM((blocks, 2, n * half, LANES), BF16),
            pltpu.VMEM((own_rank, 2 * bond_dim), BF16),
            pltpu.VMEM((own_rank, 2 * bond_dim), BF16),
            pltpu.VMEM((own_rank, 2 * bond_dim), F32),
            pltpu.VMEM((2 * own_rank, bond_dim), BF16),
            pltpu.VMEM((SUB, LANES), F32),
            pltpu.VMEM((SUB, LANES), F32),
            dma((bonds * n,)), dma((bonds * n,)),
            dma((n, CHUNKS)), dma((n, CHUNKS)),
            dma((slots, parts)), dma((slots, parts)),
            dma((blocks,)), dma((blocks,)),
            dma, dma,
            dma((blocks,)), dma((blocks,)),
            dma((slots, blocks)), dma((slots, blocks)),
            dma((slots, blocks)), dma((slots, blocks)),
            dma, dma,
        ],
        compiler_params=pltpu.CompilerParams(
            collective_id=0, has_side_effects=True, vmem_limit_bytes=62 * 1024 * 1024
        ),
        name="layer",
    )(gate, left_parts, right_site, omega)


def shards(left_site, right_site, gate, omega):
    n, bonds = lax.axis_size("row"), lax.axis_size("bond")
    rows, bond_dim = left_site.shape
    rank = omega.shape[1]
    per = rows // (2 * PARTS)
    left_parts = left_site.reshape(PARTS, per, 2, bond_dim).transpose(0, 2, 1, 3).reshape(PARTS, 2 * per, bond_dim)
    if omega.shape[0] % 16:
        omega = omega.astype(F32)
    left_blocks, right_new, odd_pair = layer(gate, left_parts, right_site, omega, n, bonds)
    left_new = left_blocks.transpose(2, 1, 0, 3).reshape(rows, rank)
    return (left_new, right_new, odd_pair)


def solution(mesh):
    split_rows = P(("bond", "row"), None)
    return jax.shard_map(
        shards,
        mesh=mesh,
        in_specs=(split_rows, split_rows, P(), split_rows),
        out_specs=(split_rows, split_rows, split_rows),
        check_vma=False,
    )
```

time: 248 us -> 152 us (0.61)
  waiting for transfers between devices: 33.2 us -> 0 us
  matrix products: 27.4 us -> 0 us
  Pallas kernels: 162 us -> 142 us
  between operations: 14.2 us -> 0.67 us
    dot_general x6 -> x0, matrix products: 27.4 us -> none  [the longest x1 5.85 us: shards(): jnp.dot(right_view, following, preferred_element_type=jnp.float32)]
    all_gather x1 -> x0, waiting for transfers between devices: 25.8 us -> none  [shards(): lax.all_gather(omega, ('bond', 'row'), axis=0, tiled=True)]
    pallas_call x3 -> x1, Pallas kernels: 162 us -> 142 us  [layer(): pl.pallas_call(functools.partial(layer_kernel, n, bonds), out_shape=(jax....]
    reduce_scatter x1 -> x0, waiting for transfers between devices: 6.77 us -> none  [shards(): lax.psum_scatter(partial, 'row', scatter_dimension=0, tiled=True)]
    reshape x4 -> x2, local copies, waits for them, and re-layouts: 5.21 us -> 2.72 us  [shards(): left_site.reshape(PARTS, per, 2, bond_dim).transpose(0, 2, 1, 3)]
  transfers between devices with their start and end apart: 2 -> 0, of which waited for: 2 -> 0; matrix products, arithmetic and copies ran while one was open for 5% -> 0% of each run, Pallas kernels for 31% -> 0%
where the time goes in v1:
time: 152 us; the launch traced here: 151 us
  Pallas kernels  142 us (93%)
  local copies, waits for them, and re-layouts  8.26 us (5%)
    pallas_call x1, Pallas kernels, layer(): pl.pallas_call(functools.partial(layer_kernel, n, bonds), out_shape=(jax....  142 us
    unnamed x7, local copies, waits for them, and re-layouts  3.54 us

profile of v1, /device:TPU:1, one launch (start us, length us, event | category | flops | bytes accessed | tf_op | source)
XLA Modules:
  0.0 151.2 jit_solution(5178005344214228326)
XLA Ops:
  0.6 1.5 reshape.15
  2.1 1.3 copy.8
  3.4 142.3 %layer.1 = (bf16[8,2,256,128]{3,2,1,0:T(8,128)(2,1)}, bf16[256,2048]{1,0:T(8,128)(2,1)}, bf16[512,2048]{1,0:T(8,128)(2,1)}) custom-call(f32[4,4]{1,0:T(4,128)} %gate_ref.1, bf16[2,256,1024]{2,1,0:T(8,128)(2,1)} %bitcast.9, bf16[256,2048]{1,0:T(8,128)(2,1)} %b_ref.1, bf16[64,1024]{1,0:T(8,128)(2,1)} %omega_ref.1), custom_call_target="tpu_custom_call" | custom-call | tf_op jit(solution)/shard_map/layer/pallas_call | solution.py:540
  145.7 0.0 copy-start.1
  145.7 2.0 %copy.9 = bf16[256,2,8,128]{3,2,1,0:T(8,128)(2,1)S(1)} copy(bf16[256,2,8,128]{3,0,1,2:T(8,128)(2,1)} %bitcast.12) | data formatting | bytes 2097152 | tf_op jit(solution)/shard_map/transpose | solution.py:595
  147.7 0.0 copy-start
  147.7 1.2 copy.12
  148.9 0.0 copy-done.1
  148.9 1.0 copy.15
  149.9 0.0 copy-done
  149.9 1.3 copy.16
Async XLA Ops:
  145.7 3.3 %copy-start.1 = (bf16[256,2048]{1,0:T(8,128)(2,1)S(1)}, bf16[256,2048]{1,0:T(8,128)(2,1)}, u32[]{:S(2)}) copy-start(bf16[256,2048]{1,0:T(8,128)(2,1)} %get-tuple-element.13) | copy-start | bytes 3145732
  147.7 2.2 %copy-start = (bf16[512,2048]{1,0:T(8,128)(2,1)S(1)}, bf16[512,2048]{1,0:T(8,128)(2,1)}, u32[]{:S(2)}) copy-start(bf16[512,2048]{1,0:T(8,128)(2,1)} %get-tuple-element.14) | copy-start | bytes 6291460

commit v2 on v1

--- a/solution.py
+++ b/solution.py
@@ -83,10 +83,24 @@
     return jnp.concatenate(rows, axis=0)
 
 
+def by_spin(rows):
+    row = lax.broadcasted_iota(jnp.int32, (rows, rows), 0)
+    col = lax.broadcasted_iota(jnp.int32, (rows, rows), 1)
+    side = rows // 2
+    return jnp.where(col == 2 * lax.rem(row, side) + lax.div(row, side), 1.0, 0.0).astype(BF16)
+
+
+def interleave(rows):
+    row = lax.broadcasted_iota(jnp.int32, (rows, rows), 0)
+    col = lax.broadcasted_iota(jnp.int32, (rows, rows), 1)
+    side = rows // 2
+    return jnp.where(col == lax.div(row, 2) + lax.rem(row, 2) * side, 1.0, 0.0).astype(BF16)
+
+
 def layer_kernel(
-    n, bonds, gate_ref, a_ref, b_ref, omega_ref, left_ref, right_ref, odd_ref,
-    a_all, b_all, omega_all, theta, w_row, w_tall, work, gram_own, gram_in, panel, wide,
-    flat, ahead, right_out, right_in, right_own, right_view, trace_own, trace_in,
+    n, bonds, gate_ref, a_ref, b_ref, omega_ref, left_out, right_ref, odd_ref,
+    a_all, a_turned, b_all, omega_all, theta, w_row, w_tall, high_all, low_all, gram_own, gram_in,
+    diagonal, pending, factor, coeff, flat, left_ref, ahead, right_out, right_in, right_own, right_view, trace_own, trace_in,
     omega_send, omega_recv, b_send, b_recv, a_send, a_recv, gram_send, gram_recv, trace_send, trace_recv,
     shift_send, shift_recv, far_send, far_recv, near_send, near_recv, right_send, right_recv,
 ):
@@ -95,10 +109,10 @@
     slots = n // 2
     slot, parity = lax.div(me, 2), lax.rem(me, 2)
     near = partner(me, 1)
-    bond_dim = a_ref.shape[2]
+    bond_dim = a_ref.shape[1]
     rank = omega_ref.shape[1]
-    part_rows = a_ref.shape[1]
-    block_rows = PARTS * part_rows
+    block_rows = a_ref.shape[0]
+    part_rows = block_rows // PARTS
     half = block_rows // 2
     own_rank = rank // n
     blocks = rank // LANES
@@ -184,7 +198,7 @@
 
     def a_copy(j, q):
         return pltpu.make_async_remote_copy(
-            src_ref=a_ref.at[q],
+            src_ref=a_ref.at[pl.ds(pl.multiple_of(q * part_rows, part_rows), part_rows), :],
             dst_ref=a_all.at[slot, q],
             send_sem=a_send.at[j, q],
             recv_sem=a_recv.at[j, q],
@@ -194,7 +208,7 @@
 
     def a_arrival(j, q):
         return pltpu.make_async_remote_copy(
-            src_ref=a_ref.at[q],
+            src_ref=a_ref.at[pl.ds(pl.multiple_of(q * part_rows, part_rows), part_rows), :],
             dst_ref=a_all.at[lax.rem(slot + slots - j, slots), q],
             send_sem=a_send.at[j, q],
             recv_sem=a_recv.at[j, q],
@@ -211,13 +225,15 @@
         for q in range(PARTS):
             a_copy(j, q).start()
 
-    a_all[slot] = a_ref[...]
+    for q in range(PARTS):
+        a_all[slot, q] = a_ref[q * part_rows:(q + 1) * part_rows, :]
     b_all[pl.ds(pl.multiple_of(me * depth, depth), depth), :] = b_ref[...]
     omega_all[pl.ds(pl.multiple_of((bond * n + me) * drawn, drawn), drawn), :] = omega_ref[...]
 
     def clear(i, carry):
         at = pl.ds(pl.multiple_of(i * LANES, LANES), LANES)
-        work[at, :] = jnp.zeros((LANES, rank), F32)
+        high_all[at, :] = jnp.zeros((LANES, rank), BF16)
+        low_all[at, :] = jnp.zeros((LANES, rank), BF16)
         gram_own[at, :] = jnp.zeros((LANES, rank), F32)
         return carry
 
@@ -252,12 +268,12 @@
         base = pl.multiple_of((at * PARTS + q) * part_rows, part_rows)
         rows = pl.ds(base, part_rows)
         side = part_rows // 2
+        a_turned[...] = dot(by_spin(part_rows), a_all[at, q]).astype(BF16)
 
         def columns(cb, carry):
             c0 = pl.multiple_of(cb * TILE, TILE)
             c1 = pl.multiple_of(bond_dim + cb * TILE, TILE)
-            block = a_all[at, q]
-            product = [dot(block, b_all[:, pl.ds(c, TILE)]) for c in (c0, c1)]
+            product = [dot(a_turned[...], b_all[:, pl.ds(c, TILE)]) for c in (c0, c1)]
             for s in range(2):
                 for t in range(2):
                     total = None
@@ -310,7 +326,6 @@
         lax.broadcasted_iota(jnp.int32, (LANES, LANES), 0)
         == lax.broadcasted_iota(jnp.int32, (LANES, LANES), 1)
     )
-    column = lax.broadcasted_iota(jnp.int32, (LANES, rank), 1)
     total = jnp.zeros((LANES, LANES), F32)
     for d in range(blocks):
         at = slice(d * LANES, (d + 1) * LANES)
@@ -375,64 +390,91 @@
             far_arrival(j, d).wait_recv()
             near_copy(j, d, parity).start()
 
-    def eliminate(d, carry):
+    column = lax.broadcasted_iota(jnp.int32, (LANES, rank), 1)
+    tall_row = lax.broadcasted_iota(jnp.int32, (rank, LANES), 0)
+    ones = jnp.where(eye, 1.0, 0.0)
+
+    def three(x):
+        high, low = split(x)
+        return jnp.concatenate([high, low, high], axis=0)
+
+    def finish(d):
         start = pl.multiple_of(d * LANES, LANES)
         here = pl.ds(start, LANES)
-        gram_copy(d).wait()
-        panel[...] = work[here, :] + jnp.where(
-            column >= start, (gram_own[here, :] + gram_in[here, :]) * scale, 0.0
-        )
-        inverse = inverse_factor(panel[:, here] + jnp.where(eye, ridge, 0.0))
-        high, low = split(inverse)
-        factor = jnp.concatenate([high, high, low], axis=1)
-        high, low = split(panel[...])
-        panel[...] = dot(factor, jnp.concatenate([high, low, high], axis=0))
-        panel[:, here] = inverse
-        high, low = split(panel[...])
-        wide[0:LANES, :] = high
-        wide[LANES:2 * LANES, :] = low
-        wide[2 * LANES:, :] = high
-
-        def update(i, carry):
-            at = pl.multiple_of(i * LANES, LANES)
-            there = pl.ds(at, LANES)
-            high, low = split(panel[:, there].T)
-            lower = jnp.concatenate([high, high, low], axis=1)
-            kept = jnp.where((column >= start) & (column < start + LANES), 0.0, work[there, :])
-            work[there, :] = kept - dot(lower, wide[...])
-            return carry
-
-        lax.fori_loop(d + 1, blocks, update, 0)
-
-        known = column < start + LANES
-        zero = jnp.zeros((LANES, rank), BF16)
-        stacked = jnp.concatenate(
-            [jnp.where(known, wide[0:LANES, :], zero), jnp.where(known, wide[LANES:2 * LANES, :], zero)], axis=0
-        )
-        both = dot(stacked, w_tall[...])
-        basis = both[:LANES, :] + both[LANES:, :]
-        flat[here, :] = basis.astype(BF16)
+        rows = dot(factor[...], three(pending[...]))
+        high_all[here, :], low_all[here, :] = split(rows)
+        for ref in (high_all, low_all):
+            ref[:, here] = jnp.where(tall_row < start, jnp.zeros((rank, LANES), BF16), ref[:, here])
+        high, low = split(jnp.where(column < start + LANES, rows, 0.0))
+        both = dot(jnp.concatenate([high, low], axis=0), w_tall[...])
+        flat[here, :] = (both[:LANES, :] + both[LANES:, :]).astype(BF16)
         side = part_rows // 2
         for q in range(PARTS):
             for s in range(2):
                 first = pl.multiple_of(slot * block_rows + q * part_rows + s * side, side)
                 left_ref[d, s, q * side:(q + 1) * side, :] = flat[here, pl.ds(first, side)].T
 
-        @pl.when(bond > 0)
+    def eliminate(d, carry):
+        start = pl.multiple_of(d * LANES, LANES)
+        here = pl.ds(start, LANES)
+        after = lax.min(d + 1, blocks - 1)
+        there = pl.ds(pl.multiple_of(after * LANES, LANES), LANES)
+
+        @pl.when(d + 1 < blocks)
         def _():
-            shift_copy(d).start()
-
-        @pl.when((bond < last) & (d > 0))
+            gram_copy(d + 1).wait()
+
+        inverse = inverse_factor(diagonal[...])
+        finish(lax.max(d - 1, 0))
+
+        known = dot(coeff[...], high_all[...])
+        known = known[:LANES, :] + known[LANES:, :] + dot(coeff[:LANES, :], low_all[...])
+        row = jnp.where(column >= start, (gram_own[here, :] + gram_in[here, :]) * scale, 0.0) - known
+        pending[...] = row
+        pending[:, here] = ones
+
+        next_high, next_low = high_all[:, there], low_all[:, there]
+        coeff[:LANES, :] = next_high.T
+        coeff[LANES:, :] = next_low.T
+        known = dot(coeff[...], next_high)
+        known = known[:LANES, :] + known[LANES:, :] + dot(coeff[:LANES, :], next_low)
+        ahead_block = (gram_own[there, there] + gram_in[there, there]) * scale - known + ones * ridge
+
+        high, low = split(inverse)
+        thrice = jnp.concatenate([high, high, low], axis=1)
+        factor[...] = thrice
+        solved = dot(thrice, three(pending[:, there]))
+        high, low = split(solved.T)
+        coeff[:LANES, here] = high
+        coeff[LANES:, here] = low
+        diagonal[...] = ahead_block - dot(jnp.concatenate([high, high, low], axis=1), three(solved))
+
+        @pl.when((bond > 0) & (d > 0))
         def _():
-            pass_on(d - 1)
+            shift_copy(d - 1).start()
 
         @pl.when((bond < last) & (d > 1))
         def _():
-            pass_near(d - 2)
+            pass_on(d - 2)
+
+        @pl.when((bond < last) & (d > 2))
+        def _():
+            pass_near(d - 3)
 
         return carry
 
+    pending[...] = jnp.zeros_like(pending)
+    factor[...] = jnp.zeros_like(factor)
+    coeff[...] = jnp.zeros_like(coeff)
+    gram_copy(0).wait()
+    diagonal[...] = (gram_own[:LANES, :LANES] + gram_in[:LANES, :LANES]) * scale + ones * ridge
     lax.fori_loop(0, blocks, eliminate, 0)
+    finish(blocks - 1)
+
+    @pl.when(bond > 0)
+    def _():
+        shift_copy(blocks - 1).start()
+
 
     right_copy = pltpu.make_async_remote_copy(
         src_ref=right_out,
@@ -459,9 +501,18 @@
 
     @pl.when(bond < last)
     def _():
-        if blocks > 1:
-            pass_near(blocks - 2)
+        pass_on(blocks - 2)
+        pass_near(blocks - 3)
+
+    turn = interleave(block_rows)
+    for d in range(0, blocks, 2):
+        pair_of = [jnp.concatenate([left_ref[d + i, 0], left_ref[d + i, 1]], axis=0) for i in range(2)]
+        left_out[:, d * LANES:(d + 2) * LANES] = dot(turn, jnp.concatenate(pair_of, axis=1)).astype(BF16)
+
+    @pl.when(bond < last)
+    def _():
         pass_on(blocks - 1)
+        pass_near(blocks - 2)
 
     right_copy.wait()
     right_scale = 1.0 / math.sqrt(2.0 * bond_dim)
@@ -469,12 +520,8 @@
 
     @pl.when(bond < last)
     def _():
-        view_rows = 2 * own_rank
-        row = lax.broadcasted_iota(jnp.int32, (view_rows, view_rows), 0)
-        col = lax.broadcasted_iota(jnp.int32, (view_rows, view_rows), 1)
-        order = jnp.where(col == lax.div(row, 2) + lax.rem(row, 2) * own_rank, 1.0, 0.0).astype(BF16)
         stacked = jnp.concatenate([right_ref[:, :bond_dim], right_ref[:, bond_dim:]], axis=0)
-        right_view[...] = dot(order, stacked).astype(BF16)
+        right_view[...] = dot(interleave(2 * own_rank), stacked).astype(BF16)
         odd_scale = 1.0 / math.sqrt(1.0 * bond_dim)
 
         def pair(d):
@@ -526,12 +573,12 @@
             a_copy(j, q).wait_send()
 
 
-def layer(gate, left_parts, right_site, omega, n, bonds):
-    parts, part_rows, bond_dim = left_parts.shape
+def layer(gate, left_site, right_site, omega, n, bonds):
+    block_rows, bond_dim = left_site.shape
+    part_rows = block_rows // PARTS
     depth = right_site.shape[0]
     drawn, rank = omega.shape
     slots = n // 2
-    block_rows = parts * part_rows
     rows = slots * block_rows
     half = block_rows // 2
     own_rank = rank // n
@@ -540,25 +587,30 @@
     return pl.pallas_call(
         functools.partial(layer_kernel, n, bonds),
         out_shape=(
-            jax.ShapeDtypeStruct((blocks, 2, half, LANES), BF16),
+            jax.ShapeDtypeStruct((block_rows, rank), BF16),
             jax.ShapeDtypeStruct((own_rank, 2 * bond_dim), BF16),
             jax.ShapeDtypeStruct((2 * own_rank, 2 * rank), BF16),
         ),
         in_specs=[pl.BlockSpec(memory_space=pltpu.SMEM)] + [pl.BlockSpec(memory_space=pltpu.VMEM)] * 3,
         out_specs=(pl.BlockSpec(memory_space=pltpu.VMEM),) * 3,
         scratch_shapes=[
-            pltpu.VMEM((slots, parts, part_rows, bond_dim), BF16),
+            pltpu.VMEM((slots, PARTS, part_rows, bond_dim), BF16),
+            pltpu.VMEM((part_rows, bond_dim), BF16),
             pltpu.VMEM((n * depth, 2 * bond_dim), BF16),
             pltpu.VMEM((bonds * n * drawn, rank), omega.dtype),
             pltpu.VMEM((rows, 2 * bond_dim), BF16),
             pltpu.VMEM((rows, rank), BF16),
             pltpu.VMEM((rank, rows), BF16),
+            pltpu.VMEM((rank, rank), BF16),
+            pltpu.VMEM((rank, rank), BF16),
             pltpu.VMEM((rank, rank), F32),
             pltpu.VMEM((rank, rank), F32),
-            pltpu.VMEM((rank, rank), F32),
+            pltpu.VMEM((LANES, LANES), F32),
             pltpu.VMEM((LANES, rank), F32),
-            pltpu.VMEM((3 * LANES, rank), BF16),
+            pltpu.VMEM((LANES, 3 * LANES), BF16),
+            pltpu.VMEM((2 * LANES, rank), BF16),
             pltpu.VMEM((rank, rows), BF16),
+            pltpu.VMEM((blocks, 2, half, LANES), BF16),
             pltpu.VMEM((blocks, 2, n * half, LANES), BF16),
             pltpu.VMEM((own_rank, 2 * bond_dim), BF16),
             pltpu.VMEM((own_rank, 2 * bond_dim), BF16),
@@ -568,7 +620,7 @@
             pltpu.VMEM((SUB, LANES), F32),
             dma((bonds * n,)), dma((bonds * n,)),
             dma((n, CHUNKS)), dma((n, CHUNKS)),
-            dma((slots, parts)), dma((slots, parts)),
+            dma((slots, PARTS)), dma((slots, PARTS)),
             dma((blocks,)), dma((blocks,)),
             dma, dma,
             dma((blocks,)), dma((blocks,)),
@@ -580,20 +632,14 @@
             collective_id=0, has_side_effects=True, vmem_limit_bytes=62 * 1024 * 1024
         ),
         name="layer",
-    )(gate, left_parts, right_site, omega)
+    )(gate, left_site, right_site, omega)
 
 
 def shards(left_site, right_site, gate, omega):
     n, bonds = lax.axis_size("row"), lax.axis_size("bond")
-    rows, bond_dim = left_site.shape
-    rank = omega.shape[1]
-    per = rows // (2 * PARTS)
-    left_parts = left_site.reshape(PARTS, per, 2, bond_dim).transpose(0, 2, 1, 3).reshape(PARTS, 2 * per, bond_dim)
     if omega.shape[0] % 16:
         omega = omega.astype(F32)
-    left_blocks, right_new, odd_pair = layer(gate, left_parts, right_site, omega, n, bonds)
-    left_new = left_blocks.transpose(2, 1, 0, 3).reshape(rows, rank)
-    return (left_new, right_new, odd_pair)
+    return layer(gate, left_site, right_site, omega, n, bonds)
 
 
 def solution(mesh):

time: 152 us -> 140 us (0.921)
  Pallas kernels: 142 us -> 135 us
  local copies, waits for them, and re-layouts: 8.26 us -> 4.71 us
    pallas_call x1, Pallas kernels: 142 us -> 135 us  [layer(): pl.pallas_call(functools.partial(layer_kernel, n, bonds), out_shape=(jax....]
    reshape x2 -> x0, local copies, waits for them, and re-layouts: 2.72 us -> none  [shards(): left_site.reshape(PARTS, per, 2, bond_dim).transpose(0, 2, 1, 3)]
    transpose x1 -> x0, local copies, waits for them, and re-layouts: 1.99 us -> none  [shards(): left_new = left_blocks.transpose(2, 1, 0, 3).reshape(rows, rank)]
where the time goes in v2:
time: 140 us
  Pallas kernels  135 us (96%)
  local copies, waits for them, and re-layouts  4.71 us (3%)
    pallas_call x1, Pallas kernels, layer(): pl.pallas_call(functools.partial(layer_kernel, n, bonds), out_shape=(jax....  135 us
    unnamed x7, local copies, waits for them, and re-layouts  4.71 us

profile of v2, /device:TPU:1, one launch (start us, length us, event | category | flops | bytes accessed | tf_op | source)
XLA Modules:
  0.0 140.1 jit_solution(10966895304208356249)
XLA Ops:
  0.6 134.7 %layer.1 = (bf16[512,1024]{1,0:T(8,128)(2,1)}, bf16[256,2048]{1,0:T(8,128)(2,1)}, bf16[512,2048]{1,0:T(8,128)(2,1)}) custom-call(f32[4,4]{1,0:T(4,128)} %gate_ref.1, bf16[512,1024]{1,0:T(8,128)(2,1)} %a_ref.1, bf16[256,2048]{1,0:T(8,128)(2,1)} %b_ref.1, bf16[64,1024]{1,0:T(8,128)(2,1)} %omega_ref.1), custom_call_target="tpu_custom_call" | custom-call | tf_op jit(solution)/shard_map/layer/pallas_call | solution.py:587
  135.3 0.0 copy-start.1
  135.3 0.0 copy-start
  135.4 2.4 %copy.10 = bf16[512,1024]{1,0:T(8,128)(2,1)} copy(bf16[512,1024]{1,0:T(8,128)(2,1)} %get-tuple-element.6) | data formatting | bytes 2097152
  137.8 0.0 copy-done.1
  137.8 1.0 copy.11
  138.7 0.0 copy-done
  138.7 1.3 copy.12
Async XLA Ops:
  135.3 2.4 %copy-start.1 = (bf16[256,2048]{1,0:T(8,128)(2,1)S(1)}, bf16[256,2048]{1,0:T(8,128)(2,1)}, u32[]{:S(2)}) copy-start(bf16[256,2048]{1,0:T(8,128)(2,1)} %get-tuple-element.7) | copy-start | bytes 3145732
  135.3 3.4 %copy-start = (bf16[512,2048]{1,0:T(8,128)(2,1)S(1)}, bf16[512,2048]{1,0:T(8,128)(2,1)}, u32[]{:S(2)}) copy-start(bf16[512,2048]{1,0:T(8,128)(2,1)} %get-tuple-element.8) | copy-start | bytes 6291460

commit v3 on v2

--- a/solution.py
+++ b/solution.py
@@ -44,9 +44,8 @@
     groups = LANES // SUB
     lane = lax.broadcasted_iota(jnp.int32, (SUB, LANES), 1)
     sub = lax.broadcasted_iota(jnp.int32, (SUB, LANES), 0)
-    left = [block[g * SUB:(g + 1) * SUB, :] for g in range(groups)]
-    right = [jnp.where(lane == sub + g * SUB, 1.0, 0.0) for g in range(groups)]
-    rows = []
+    rows = [block[g * SUB:(g + 1) * SUB, :] for g in range(groups)]
+    finished = []
 
     def over_lanes(x, column):
         return jnp.broadcast_to(x[:, column:column + 1], (SUB, LANES))
@@ -54,33 +53,52 @@
     def over_rows(x, row):
         return jnp.broadcast_to(x[row:row + 1, :], (SUB, LANES))
 
-    for g in range(groups):
-        a, e = left[g], right[g]
-        cols = [over_lanes(a, g * SUB + c) for c in range(SUB)]
-        finished = jnp.zeros_like(e)
+    def inside(g):
+        return (lane >= g * SUB) & (lane < (g + 1) * SUB)
+
+    def columns(x, g):
+        return [over_lanes(x, g * SUB + c) for c in range(SUB)]
+
+    def pivots(g, cols, low=None, after=None):
+        x = jnp.where(inside(g), jnp.where(lane == sub + g * SUB, 1.0, 0.0), rows[g])
+        out = jnp.zeros_like(x)
         for k in range(SUB):
             here = sub == k
             root = lax.rsqrt(over_rows(cols[k], k))
             inverse = root * root
-            factor = cols[k] * inverse
-            row_a, row_e = over_rows(a, k), over_rows(e, k)
-            finished = jnp.where(here, row_e * root, finished)
-            a = jnp.where(here, row_a * inverse, a - factor * row_a)
-            e = jnp.where(here, row_e * inverse, e - factor * row_e)
+            row = over_rows(x, k)
+            out = jnp.where(here, row * root, out)
+            ratio = cols[k] * inverse
+            x = jnp.where(here, row * inverse, x - ratio * row)
+            tops = {c: over_rows(cols[c], k) for c in range(k + 1, SUB)}
             for c in range(k + 1, SUB):
-                row_c = over_rows(cols[c], k)
-                cols[c] = jnp.where(here, row_c * inverse, cols[c] - factor * row_c)
-        rows.append(finished)
-        if g + 1 == groups:
-            break
-        wide_a = [over_rows(a, k) for k in range(SUB)]
-        wide_e = [over_rows(e, k) for k in range(SUB)]
-        for i in range(g + 1, groups):
-            coeff = [over_lanes(left[i], g * SUB + c) for c in range(SUB)]
-            for c in range(SUB):
-                left[i] = left[i] - coeff[c] * wide_a[c]
-                right[i] = right[i] - coeff[c] * wide_e[c]
-    return jnp.concatenate(rows, axis=0)
+                cols[c] = jnp.where(here, tops[c] * inverse, cols[c] - ratio * tops[c])
+            if low is not None:
+                below = low[k] * inverse
+                for c in range(SUB):
+                    after[c] = after[c] - below * over_rows(low[k], c)
+                for c in range(k + 1, SUB):
+                    low[c] = low[c] - below * tops[c]
+        finished.append(jnp.where(lane <= sub + g * SUB, out, 0.0))
+        return [over_rows(x, k) for k in range(SUB)]
+
+    def remove(i, g, coeff, wide):
+        rest = jnp.where(inside(g), 0.0, rows[i])
+        for c in range(SUB):
+            rest = rest - coeff[c] * wide[c]
+        rows[i] = rest
+
+    for g in range(0, groups, 2):
+        cols = columns(rows[g], g)
+        low, after = columns(rows[g + 1], g), columns(rows[g + 1], g + 1)
+        wide = pivots(g, cols, list(low), after)
+        remove(g + 1, g, low, wide)
+        for i in range(g + 2, groups):
+            remove(i, g, columns(rows[i], g), wide)
+        wide = pivots(g + 1, after)
+        for i in range(g + 2, groups):
+            remove(i, g + 1, columns(rows[i], g + 1), wide)
+    return jnp.concatenate(finished, axis=0)
 
 
 def by_spin(rows):
@@ -100,7 +118,7 @@
 def layer_kernel(
     n, bonds, gate_ref, a_ref, b_ref, omega_ref, left_out, right_ref, odd_ref,
     a_all, a_turned, b_all, omega_all, theta, w_row, w_tall, high_all, low_all, gram_own, gram_in,
-    diagonal, pending, factor, coeff, flat, left_ref, ahead, right_out, right_in, right_own, right_view, trace_own, trace_in,
+    diagonal, pending, factor, coeff, flat, left_ref, ahead, right_out, right_in, right_view, trace_own, trace_in,
     omega_send, omega_recv, b_send, b_recv, a_send, a_recv, gram_send, gram_recv, trace_send, trace_recv,
     shift_send, shift_recv, far_send, far_recv, near_send, near_recv, right_send, right_recv,
 ):
@@ -398,23 +416,22 @@
         high, low = split(x)
         return jnp.concatenate([high, low, high], axis=0)
 
-    def finish(d):
+    def finish(d, deep):
         start = pl.multiple_of(d * LANES, LANES)
         here = pl.ds(start, LANES)
         rows = dot(factor[...], three(pending[...]))
         high_all[here, :], low_all[here, :] = split(rows)
         for ref in (high_all, low_all):
-            ref[:, here] = jnp.where(tall_row < start, jnp.zeros((rank, LANES), BF16), ref[:, here])
-        high, low = split(jnp.where(column < start + LANES, rows, 0.0))
-        both = dot(jnp.concatenate([high, low], axis=0), w_tall[...])
-        flat[here, :] = (both[:LANES, :] + both[LANES:, :]).astype(BF16)
+            ref[:deep, here] = jnp.where(tall_row[:deep] < start, jnp.zeros((deep, LANES), BF16), ref[:deep, here])
+        high, low = split(jnp.where(column[:, :deep] < start + LANES, rows[:, :deep], 0.0))
+        flat[here, :] = (dot(high, w_tall[:deep, :]) + dot(low, w_tall[:deep, :])).astype(BF16)
         side = part_rows // 2
         for q in range(PARTS):
             for s in range(2):
                 first = pl.multiple_of(slot * block_rows + q * part_rows + s * side, side)
                 left_ref[d, s, q * side:(q + 1) * side, :] = flat[here, pl.ds(first, side)].T
 
-    def eliminate(d, carry):
+    def eliminate(deep, d, carry):
         start = pl.multiple_of(d * LANES, LANES)
         here = pl.ds(start, LANES)
         after = lax.min(d + 1, blocks - 1)
@@ -425,19 +442,25 @@
             gram_copy(d + 1).wait()
 
         inverse = inverse_factor(diagonal[...])
-        finish(lax.max(d - 1, 0))
-
-        known = dot(coeff[...], high_all[...])
-        known = known[:LANES, :] + known[LANES:, :] + dot(coeff[:LANES, :], low_all[...])
+        finish(lax.max(d - 1, 0), deep)
+
+        known = (
+            dot(coeff[:LANES, :deep], high_all[:deep, :])
+            + dot(coeff[LANES:, :deep], high_all[:deep, :])
+            + dot(coeff[:LANES, :deep], low_all[:deep, :])
+        )
         row = jnp.where(column >= start, (gram_own[here, :] + gram_in[here, :]) * scale, 0.0) - known
         pending[...] = row
         pending[:, here] = ones
 
-        next_high, next_low = high_all[:, there], low_all[:, there]
-        coeff[:LANES, :] = next_high.T
-        coeff[LANES:, :] = next_low.T
-        known = dot(coeff[...], next_high)
-        known = known[:LANES, :] + known[LANES:, :] + dot(coeff[:LANES, :], next_low)
+        next_high, next_low = high_all[:deep, there], low_all[:deep, there]
+        coeff[:LANES, :deep] = next_high.T
+        coeff[LANES:, :deep] = next_low.T
+        known = (
+            dot(coeff[:LANES, :deep], next_high)
+            + dot(coeff[LANES:, :deep], next_high)
+            + dot(coeff[:LANES, :deep], next_low)
+        )
         ahead_block = (gram_own[there, there] + gram_in[there, there]) * scale - known + ones * ridge
 
         high, low = split(inverse)
@@ -468,8 +491,9 @@
     coeff[...] = jnp.zeros_like(coeff)
     gram_copy(0).wait()
     diagonal[...] = (gram_own[:LANES, :LANES] + gram_in[:LANES, :LANES]) * scale + ones * ridge
-    lax.fori_loop(0, blocks, eliminate, 0)
-    finish(blocks - 1)
+    lax.fori_loop(0, blocks // 2, functools.partial(eliminate, rank // 2), 0)
+    lax.fori_loop(blocks // 2, blocks, functools.partial(eliminate, rank), 0)
+    finish(blocks - 1, rank)
 
     @pl.when(bond > 0)
     def _():
@@ -485,19 +509,26 @@
         device_id_type=MESH,
     )
 
-    def project(who, target):
+    right_scale = 1.0 / math.sqrt(2.0 * bond_dim)
+
+    def project(who, store):
         ranks = pl.ds(pl.multiple_of(who * own_rank, own_rank), own_rank)
 
         def columns(cb, carry):
             at = pl.ds(pl.multiple_of(cb * TILE, TILE), TILE)
-            target[:, at] = dot(flat[ranks, :], theta[:, at]).astype(target.dtype)
+            store(at, dot(flat[ranks, :], theta[:, at]) * right_scale)
             return carry
 
         lax.fori_loop(0, 2 * bond_dim // TILE, columns, 0)
 
-    project(near, right_out)
+    def give(at, value):
+        right_out[:, at] = value.astype(BF16)
+
+    def keep(at, value):
+        right_ref[:, at] = (value + right_in[:, at].astype(F32)).astype(BF16)
+
+    project(near, give)
     right_copy.start()
-    project(me, right_own)
 
     @pl.when(bond < last)
     def _():
@@ -509,14 +540,14 @@
         pair_of = [jnp.concatenate([left_ref[d + i, 0], left_ref[d + i, 1]], axis=0) for i in range(2)]
         left_out[:, d * LANES:(d + 2) * LANES] = dot(turn, jnp.concatenate(pair_of, axis=1)).astype(BF16)
 
+    right_copy.wait()
+    project(me, keep)
+
     @pl.when(bond < last)
     def _():
         pass_on(blocks - 1)
         pass_near(blocks - 2)
 
-    right_copy.wait()
-    right_scale = 1.0 / math.sqrt(2.0 * bond_dim)
-    right_ref[...] = ((right_own[...] + right_in[...].astype(F32)) * right_scale).astype(BF16)
 
     @pl.when(bond < last)
     def _():
@@ -614,7 +645,6 @@
             pltpu.VMEM((blocks, 2, n * half, LANES), BF16),
             pltpu.VMEM((own_rank, 2 * bond_dim), BF16),
             pltpu.VMEM((own_rank, 2 * bond_dim), BF16),
-            pltpu.VMEM((own_rank, 2 * bond_dim), F32),
             pltpu.VMEM((2 * own_rank, bond_dim), BF16),
             pltpu.VMEM((SUB, LANES), F32),
             pltpu.VMEM((SUB, LANES), F32),
@@ -629,7 +659,7 @@
             dma, dma,
         ],
         compiler_params=pltpu.CompilerParams(
-            collective_id=0, has_side_effects=True, vmem_limit_bytes=62 * 1024 * 1024
+            collective_id=0, has_side_effects=True, vmem_limit_bytes=(49 if omega.dtype == BF16 else 61) * 1024 * 1024
         ),
         name="layer",
     )(gate, left_site, right_site, omega)

time: 140 us -> 134 us (0.957)
  Pallas kernels: 135 us -> 126 us
  local copies, waits for them, and re-layouts: 4.71 us -> 7.33 us
    pallas_call x1, Pallas kernels: 135 us -> 126 us  [layer(): pl.pallas_call(functools.partial(layer_kernel, n, bonds), out_shape=(jax....]
    unnamed x7 -> x13, local copies, waits for them, and re-layouts: 4.71 us -> 7.33 us
where the time goes in v3:
time: 134 us
  Pallas kernels  126 us (94%)
  local copies, waits for them, and re-layouts  7.33 us (5%)
    pallas_call x1, Pallas kernels, layer(): pl.pallas_call(functools.partial(layer_kernel, n, bonds), out_shape=(jax....  126 us
    unnamed x13, local copies, waits for them, and re-layouts  7.33 us

profile of v3, /device:TPU:1, one launch (start us, length us, event | category | flops | bytes accessed | tf_op | source)
XLA Modules:
  0.0 134.1 jit_solution(7815428148633760508)
XLA Ops:
  0.6 0.0 copy-start
  0.6 1.2 copy-done
  1.9 0.0 copy-start.1
  1.9 1.2 copy-done.1
  3.1 0.0 copy-start.2
  3.1 0.9 copy-done.2
  4.0 0.0 copy-start.3
  4.0 0.7 copy-done.3
  4.7 126.1 %layer.1 = (bf16[512,1024]{1,0:T(8,128)(2,1)S(1)}, bf16[256,2048]{1,0:T(8,128)(2,1)S(1)}, bf16[512,2048]{1,0:T(8,128)(2,1)}) custom-call(f32[4,4]{1,0:T(4,128)S(1)} %copy-done.3, bf16[512,1024]{1,0:T(8,128)(2,1)S(1)} %copy-done, bf16[256,2048]{1,0:T(8,128)(2,1)S(1)} %copy-done.1, bf16[64,1024]{1,0:T(8,128)(2,1)S(1)} %copy-done.2), custom_call_target="tpu_custom_call" | custom-call | tf_op jit(solution)/shard_map/layer/pallas_call | solution.py:618
  130.8 0.0 copy-start.4
  130.8 1.0 copy.10
  131.8 1.0 copy.11
  132.8 0.0 copy-done.4
  132.8 1.3 copy.12
Async XLA Ops:
  0.6 1.2 copy-start
  1.9 1.2 copy-start.1
  3.1 0.9 copy-start.2
  4.0 0.7 copy-start.3
  130.8 2.0 %copy-start.4 = (bf16[512,2048]{1,0:T(8,128)(2,1)S(1)}, bf16[512,2048]{1,0:T(8,128)(2,1)}, u32[]{:S(2)}) copy-start(bf16[512,2048]{1,0:T(8,128)(2,1)} %get-tuple-element.8) | copy-start | bytes 6291460

commit v4 on v3

--- a/solution.py
+++ b/solution.py
@@ -121,6 +121,7 @@
     diagonal, pending, factor, coeff, flat, left_ref, ahead, right_out, right_in, right_view, trace_own, trace_in,
     omega_send, omega_recv, b_send, b_recv, a_send, a_recv, gram_send, gram_recv, trace_send, trace_recv,
     shift_send, shift_recv, far_send, far_recv, near_send, near_recv, right_send, right_recv,
+    direct_send, direct_recv,
 ):
     bond, me = lax.axis_index("bond"), lax.axis_index("row")
     last = bonds - 1
@@ -157,8 +158,9 @@
         greeted += 1
     for way in (1, last):
         to = lax.rem(bond + way, bonds)
-        pl.semaphore_signal(barrier, inc=1, device_id={"bond": to}, device_id_type=MESH)
-        greeted += 1
+        for j in range(slots):
+            pl.semaphore_signal(barrier, inc=1, device_id={"bond": to, "row": peer(j)}, device_id_type=MESH)
+            greeted += 1
     pl.semaphore_wait(barrier, greeted)
 
     hops = [("row", s) for s in row_steps[:-1]] + [("bond", s) for s in bond_steps] + [("row", 1)]
@@ -338,8 +340,6 @@
         device_id={"row": near},
         device_id_type=MESH,
     )
-    for i in range(blocks):
-        gram_copy(i).start()
     eye = (
         lax.broadcasted_iota(jnp.int32, (LANES, LANES), 0)
         == lax.broadcasted_iota(jnp.int32, (LANES, LANES), 1)
@@ -350,6 +350,8 @@
         total = total + jnp.where(eye, gram_own[at, at], 0.0)
     trace_own[...] = jnp.broadcast_to(jnp.sum(total, keepdims=True), (SUB, LANES))
     trace_copy.start()
+    for i in range(blocks):
+        gram_copy(i).start()
     scale = 1.0 / (2.0 * bond_dim)
     trace_copy.wait()
     ridge = (trace_own[0:1, 0:1] + trace_in[0:1, 0:1]) * (scale * 0.01 / rank)
@@ -394,6 +396,26 @@
             send_sem=near_send.at[j, d],
             recv_sem=near_recv.at[j, d],
             device_id={"row": near},
+            device_id_type=MESH,
+        )
+
+    def direct_copy(j):
+        return pltpu.make_async_remote_copy(
+            src_ref=left_ref.at[blocks - 1],
+            dst_ref=ahead_at(blocks - 1, me),
+            send_sem=direct_send.at[j],
+            recv_sem=direct_recv.at[j],
+            device_id={"bond": lax.max(bond - 1, 0), "row": peer(j)},
+            device_id_type=MESH,
+        )
+
+    def direct_arrival(j):
+        return pltpu.make_async_remote_copy(
+            src_ref=left_ref.at[blocks - 1],
+            dst_ref=ahead_at(blocks - 1, source(j, parity)),
+            send_sem=direct_send.at[j],
+            recv_sem=direct_recv.at[j],
+            device_id={"bond": lax.max(bond - 1, 0), "row": peer(j)},
             device_id_type=MESH,
         )
 
@@ -424,7 +446,8 @@
         for ref in (high_all, low_all):
             ref[:deep, here] = jnp.where(tall_row[:deep] < start, jnp.zeros((deep, LANES), BF16), ref[:deep, here])
         high, low = split(jnp.where(column[:, :deep] < start + LANES, rows[:, :deep], 0.0))
-        flat[here, :] = (dot(high, w_tall[:deep, :]) + dot(low, w_tall[:deep, :])).astype(BF16)
+        own = pl.ds(pl.multiple_of(slot * block_rows, block_rows), block_rows)
+        flat[here, own] = (dot(high, w_tall[:deep, own]) + dot(low, w_tall[:deep, own])).astype(BF16)
         side = part_rows // 2
         for q in range(PARTS):
             for s in range(2):
@@ -498,6 +521,8 @@
     @pl.when(bond > 0)
     def _():
         shift_copy(blocks - 1).start()
+        for j in range(1, slots):
+            direct_copy(j).start()
 
 
     right_copy = pltpu.make_async_remote_copy(
@@ -527,6 +552,13 @@
     def keep(at, value):
         right_ref[:, at] = (value + right_in[:, at].astype(F32)).astype(BF16)
 
+    pair_ranks = pl.ds(pl.multiple_of(slot * 2 * own_rank, 2 * own_rank), 2 * own_rank)
+    for j in range(1, slots):
+        at = pl.ds(pl.multiple_of(lax.rem(slot + j, slots) * block_rows, block_rows), block_rows)
+        flat[pair_ranks, at] = (
+            dot(high_all[pair_ranks, :], w_tall[:, at]) + dot(low_all[pair_ranks, :], w_tall[:, at])
+        ).astype(BF16)
+
     project(near, give)
     right_copy.start()
 
@@ -545,9 +577,9 @@
 
     @pl.when(bond < last)
     def _():
-        pass_on(blocks - 1)
         pass_near(blocks - 2)
-
+        shift_copy(blocks - 1).wait_recv()
+        near_copy(0, blocks - 1, parity).start()
 
     @pl.when(bond < last)
     def _():
@@ -568,15 +600,22 @@
             return carry
 
         lax.fori_loop(0, blocks - 1, pairs, 0)
-        pass_near(blocks - 1)
+        for j in range(1, slots):
+            direct_arrival(j).wait_recv()
+            near_copy(j, blocks - 1, parity).start()
         pair(blocks - 1)
 
         def sent(d, carry):
-            for j in range(1, slots):
-                far_copy(j, d).wait_send()
             for j in range(slots):
                 near_copy(j, d, parity).wait_send()
             return carry
+
+        def sent_far(d, carry):
+            for j in range(1, slots):
+                far_copy(j, d).wait_send()
+            return carry
+
+        lax.fori_loop(0, blocks - 1, sent_far, 0)
 
         lax.fori_loop(0, blocks, sent, 0)
 
@@ -591,6 +630,8 @@
             return carry
 
         lax.fori_loop(0, blocks, sent, 0)
+        for j in range(1, slots):
+            direct_copy(j).wait_send()
 
     for mask in [0] + omega_order:
         for bit in lower_bits(mask):
@@ -657,6 +698,7 @@
             dma((slots, blocks)), dma((slots, blocks)),
             dma((slots, blocks)), dma((slots, blocks)),
             dma, dma,
+            dma((slots,)), dma((slots,)),
         ],
         compiler_params=pltpu.CompilerParams(
             collective_id=0, has_side_effects=True, vmem_limit_bytes=(49 if omega.dtype == BF16 else 61) * 1024 * 1024

time: 134 us -> 131 us (0.978)
  Pallas kernels: 126 us -> 123 us
    pallas_call x1, Pallas kernels: 126 us -> 123 us  [layer(): pl.pallas_call(functools.partial(layer_kernel, n, bonds), out_shape=(jax....]
where the time goes in v4:
time: 131 us
  Pallas kernels  123 us (94%)
  local copies, waits for them, and re-layouts  7.33 us (6%)
    pallas_call x1, Pallas kernels, layer(): pl.pallas_call(functools.partial(layer_kernel, n, bonds), out_shape=(jax....  123 us
    unnamed x13, local copies, waits for them, and re-layouts  7.33 us

profile of v4, /device:TPU:1, one launch (start us, length us, event | category | flops | bytes accessed | tf_op | source)
XLA Modules:
  0.0 131.0 jit_solution(81785486392655901)
XLA Ops:
  0.6 0.0 copy-start
  0.6 1.2 copy-done
  1.9 0.0 copy-start.1
  1.9 1.2 copy-done.1
  3.1 0.0 copy-start.2
  3.1 0.9 copy-done.2
  4.0 0.0 copy-start.3
  4.0 0.7 copy-done.3
  4.7 123.0 %layer.1 = (bf16[512,1024]{1,0:T(8,128)(2,1)S(1)}, bf16[256,2048]{1,0:T(8,128)(2,1)S(1)}, bf16[512,2048]{1,0:T(8,128)(2,1)}) custom-call(f32[4,4]{1,0:T(4,128)S(1)} %copy-done.3, bf16[512,1024]{1,0:T(8,128)(2,1)S(1)} %copy-done, bf16[256,2048]{1,0:T(8,128)(2,1)S(1)} %copy-done.1, bf16[64,1024]{1,0:T(8,128)(2,1)S(1)} %copy-done.2), custom_call_target="tpu_custom_call" | custom-call | tf_op jit(solution)/shard_map/layer/pallas_call | solution.py:659
  127.7 0.0 copy-start.4
  127.7 1.0 copy.10
  128.7 1.0 copy.11
  129.6 0.0 copy-done.4
  129.7 1.3 %copy.12 = bf16[512,2048]{1,0:T(8,128)(2,1)} copy(bf16[512,2048]{1,0:T(8,128)(2,1)S(1)} %copy-done.4) | data formatting | bytes 4194304
Async XLA Ops:
  0.6 1.2 copy-start
  1.9 1.2 copy-start.1
  3.1 0.9 copy-start.2
  4.0 0.7 copy-start.3
  127.7 2.0 %copy-start.4 = (bf16[512,2048]{1,0:T(8,128)(2,1)S(1)}, bf16[512,2048]{1,0:T(8,128)(2,1)}, u32[]{:S(2)}) copy-start(bf16[512,2048]{1,0:T(8,128)(2,1)} %get-tuple-element.8) | copy-start | bytes 6291460

commit v5 on v4

--- a/solution.py
+++ b/solution.py
@@ -116,12 +116,12 @@
 
 
 def layer_kernel(
-    n, bonds, gate_ref, a_ref, b_ref, omega_ref, left_out, right_ref, odd_ref,
+    n, bonds, gate_hbm, a_ref, b_ref, omega_ref, left_out, right_ref, odd_ref,
     a_all, a_turned, b_all, omega_all, theta, w_row, w_tall, high_all, low_all, gram_own, gram_in,
     diagonal, pending, factor, coeff, flat, left_ref, ahead, right_out, right_in, right_view, trace_own, trace_in,
     omega_send, omega_recv, b_send, b_recv, a_send, a_recv, gram_send, gram_recv, trace_send, trace_recv,
     shift_send, shift_recv, far_send, far_recv, near_send, near_recv, right_send, right_recv,
-    direct_send, direct_recv,
+    direct_send, direct_recv, load_sem, gate_sem, gate_ref,
 ):
     bond, me = lax.axis_index("bond"), lax.axis_index("row")
     last = bonds - 1
@@ -147,6 +147,20 @@
 
     row_steps, bond_steps = distances(n), distances(bonds)
 
+    own_depth = pl.ds(pl.multiple_of(me * depth, depth), depth)
+    own_drawn = pl.ds(pl.multiple_of((bond * n + me) * drawn, drawn), drawn)
+    loads = [
+        pltpu.make_async_copy(omega_ref, omega_all.at[own_drawn, :], load_sem.at[0]),
+        pltpu.make_async_copy(b_ref, b_all.at[own_depth, :], load_sem.at[1]),
+    ]
+    for q in range(PARTS):
+        rows = pl.ds(q * part_rows, part_rows)
+        loads.append(pltpu.make_async_copy(a_ref.at[rows, :], a_all.at[slot, q], load_sem.at[2 + q]))
+    gate_load = pltpu.make_async_copy(gate_hbm, gate_ref, gate_sem)
+    for load in loads:
+        load.start()
+    gate_load.start()
+
     barrier = pltpu.get_barrier_semaphore()
     greeted = 0
     for j in range(1, n):
@@ -182,7 +196,7 @@
         axis, s = hop_of[bit]
         to = partner(me if axis == "row" else bond, s)
         return pltpu.make_async_remote_copy(
-            src_ref=omega_slot(mask) if mask else omega_ref,
+            src_ref=omega_slot(mask),
             dst_ref=omega_slot(mask),
             send_sem=omega_send.at[mask + bit],
             recv_sem=omega_recv.at[mask + bit],
@@ -203,7 +217,7 @@
         start = pl.multiple_of(at * depth + k * piece, piece)
         target = b_all.at[pl.ds(start, piece), :]
         return pltpu.make_async_remote_copy(
-            src_ref=target if mask else b_ref.at[k * piece:(k + 1) * piece, :],
+            src_ref=target,
             dst_ref=target,
             send_sem=b_send.at[mask + s, k],
             recv_sem=b_recv.at[mask + s, k],
@@ -218,7 +232,7 @@
 
     def a_copy(j, q):
         return pltpu.make_async_remote_copy(
-            src_ref=a_ref.at[pl.ds(pl.multiple_of(q * part_rows, part_rows), part_rows), :],
+            src_ref=a_all.at[slot, q],
             dst_ref=a_all.at[slot, q],
             send_sem=a_send.at[j, q],
             recv_sem=a_recv.at[j, q],
@@ -228,7 +242,7 @@
 
     def a_arrival(j, q):
         return pltpu.make_async_remote_copy(
-            src_ref=a_ref.at[pl.ds(pl.multiple_of(q * part_rows, part_rows), part_rows), :],
+            src_ref=a_all.at[slot, q],
             dst_ref=a_all.at[lax.rem(slot + slots - j, slots), q],
             send_sem=a_send.at[j, q],
             recv_sem=a_recv.at[j, q],
@@ -236,19 +250,18 @@
             device_id_type=MESH,
         )
 
+    loads[0].wait()
     for bit in bits:
         omega_copy(0, bit).start()
+    loads[1].wait()
     for s in row_steps:
         for k in range(CHUNKS):
             b_copy(0, s, k).start()
-    for j in range(1, slots):
-        for q in range(PARTS):
+    for q in range(PARTS):
+        loads[2 + q].wait()
+        for j in range(1, slots):
             a_copy(j, q).start()
-
-    for q in range(PARTS):
-        a_all[slot, q] = a_ref[q * part_rows:(q + 1) * part_rows, :]
-    b_all[pl.ds(pl.multiple_of(me * depth, depth), depth), :] = b_ref[...]
-    omega_all[pl.ds(pl.multiple_of((bond * n + me) * drawn, drawn), drawn), :] = omega_ref[...]
+    gate_load.wait()
 
     def clear(i, carry):
         at = pl.ds(pl.multiple_of(i * LANES, LANES), LANES)
@@ -663,7 +676,7 @@
             jax.ShapeDtypeStruct((own_rank, 2 * bond_dim), BF16),
             jax.ShapeDtypeStruct((2 * own_rank, 2 * rank), BF16),
         ),
-        in_specs=[pl.BlockSpec(memory_space=pltpu.SMEM)] + [pl.BlockSpec(memory_space=pltpu.VMEM)] * 3,
+        in_specs=[pl.BlockSpec(memory_space=pltpu.HBM)] * 4,
         out_specs=(pl.BlockSpec(memory_space=pltpu.VMEM),) * 3,
         scratch_shapes=[
             pltpu.VMEM((slots, PARTS, part_rows, bond_dim), BF16),
@@ -699,9 +712,11 @@
             dma((slots, blocks)), dma((slots, blocks)),
             dma, dma,
             dma((slots,)), dma((slots,)),
+            dma((2 + PARTS,)), dma,
+            pltpu.SMEM(gate.shape, F32),
         ],
         compiler_params=pltpu.CompilerParams(
-            collective_id=0, has_side_effects=True, vmem_limit_bytes=(49 if omega.dtype == BF16 else 61) * 1024 * 1024
+            collective_id=0, has_side_effects=True, vmem_limit_bytes=62 * 1024 * 1024
         ),
         name="layer",
     )(gate, left_site, right_site, omega)

time: 131 us -> 129 us (0.985)
  local copies, waits for them, and re-layouts: 7.33 us -> 4.71 us
    unnamed x13 -> x7, local copies, waits for them, and re-layouts: 7.33 us -> 4.71 us
where the time goes in v5:
time: 129 us; the launch traced here: 128 us
  Pallas kernels  123 us (95%)
  local copies, waits for them, and re-layouts  4.71 us (4%)
    pallas_call x1, Pallas kernels, layer(): pl.pallas_call(functools.partial(layer_kernel, n, bonds), out_shape=(jax....  123 us
    unnamed x7, local copies, waits for them, and re-layouts  4.71 us

profile of v5, /device:TPU:1, one launch (start us, length us, event | category | flops | bytes accessed | tf_op | source)
XLA Modules:
  0.0 128.5 jit_solution(9352239198836858631)
XLA Ops:
  0.6 123.1 %layer.1 = (bf16[512,1024]{1,0:T(8,128)(2,1)}, bf16[256,2048]{1,0:T(8,128)(2,1)}, bf16[512,2048]{1,0:T(8,128)(2,1)}) custom-call(f32[4,4]{1,0:T(4,128)} %gate_hbm.1, bf16[512,1024]{1,0:T(8,128)(2,1)} %a_ref.1, bf16[256,2048]{1,0:T(8,128)(2,1)} %b_ref.1, bf16[64,1024]{1,0:T(8,128)(2,1)} %omega_ref.1), custom_call_target="tpu_custom_call" | custom-call | tf_op jit(solution)/shard_map/layer/pallas_call | solution.py:672
  123.8 0.0 copy-start.1
  123.8 0.0 copy-start
  123.8 2.4 %copy.10 = bf16[512,1024]{1,0:T(8,128)(2,1)} copy(bf16[512,1024]{1,0:T(8,128)(2,1)} %get-tuple-element.6) | data formatting | bytes 2097152
  126.2 0.0 copy-done.1
  126.2 1.0 copy.11
  127.2 0.0 copy-done
  127.2 1.3 %copy.12 = bf16[512,2048]{1,0:T(8,128)(2,1)} copy(bf16[512,2048]{1,0:T(8,128)(2,1)S(1)} %copy-done) | data formatting | bytes 4194304
Async XLA Ops:
  123.8 2.4 %copy-start.1 = (bf16[256,2048]{1,0:T(8,128)(2,1)S(1)}, bf16[256,2048]{1,0:T(8,128)(2,1)}, u32[]{:S(2)}) copy-start(bf16[256,2048]{1,0:T(8,128)(2,1)} %get-tuple-element.7) | copy-start | bytes 3145732
  123.8 3.4 %copy-start = (bf16[512,2048]{1,0:T(8,128)(2,1)S(1)}, bf16[512,2048]{1,0:T(8,128)(2,1)}, u32[]{:S(2)}) copy-start(bf16[512,2048]{1,0:T(8,128)(2,1)} %get-tuple-element.8) | copy-start | bytes 6291460
